TPU v7x, 256 devices: a whole 4x4x8 slice. The times are simulated.
256 devices in a mesh: tok: 64 (over x, z, core), tp: 4 (over y).
Axes of the slice: x: 4, y: 4, z: 8, core: 2. Of those that a mesh axis runs over, the one named last changes fastest.
Arguments:
- resid: bfloat16 [8192, 8192], P('tok', 'tp'), may hold values from -7 to 7
- norm_gain: float32 [8192], P('tp'), may hold values from 0.5 to 1.5
- head_in: bfloat16 [8192, 2048], P('tp'), may hold values from -0.088388348 to 0.088388348
- head_bias: float32 [2048], replicated, may hold values from -3 to 3
- head_out: float32 [16, 128], replicated, may hold values from -0.26516504 to 0.26516504
- targets: float32 [8192, 16], P('tok'), may hold values from -12 to 12
- label_mask: int32 [8192, 16], P('tok'), may hold values 0 or 1
- obj_weight: int32 [16], replicated, may hold values from 1 to 16
Outputs:
- resid_grad: bfloat16 [8192, 8192], P('tok', 'tp')
- gain_grad: float32 [8192], P('tp')
- head_in_grad: float32 [8192, 2048], P('tp', 'tok')
- head_bias_grad: float32 [2048], replicated
All inputs are finite; a program needn't handle non-finite values. No bound on the sum of `label_mask` on one device may be relied on, other than what follows from the above.
Results may differ from a plain program's by a relative error of at most 0.0078.
Values may be sent and summed in bfloat16 or wider, within the bound.
A program may use at most 128 MiB of HBM per device.

v0:
```python
import functools

import jax
import jax.numpy as jnp
from jax import lax
from jax.sharding import Mesh
from jax.sharding import PartitionSpec as P

D = 8192
TOK = ("tok_0", "tok_1", "tok_2")
TOK_TP = ("tok_0", "tok_1", "tok_2", "tp")


norm_eps = 1e-05
grad_eps = 1e-06
denominator = 8.0


def sent_to_all(array, axis):
    peers = lax.axis_size(axis)
    return lax.all_to_all(
        jnp.broadcast_to(array[None], (peers, *array.shape)), axis, 0, 0, tiled=True
    )


def over_copies(array, axis):
    everything = sent_to_all(array, axis)
    return jnp.sum(everything, axis=0)


def in_blocks(array, dim, peers):
    dims = array.shape
    tiles = array.reshape(*dims[:dim], peers, dims[dim] // peers, *dims[dim + 1 :])
    return jnp.moveaxis(tiles, dim, 0)


def summed_on_arrival(array, axis, dim):
    peers = lax.axis_size(axis)
    tiles = lax.all_to_all(in_blocks(array, dim, peers), axis, 0, 0, tiled=True)
    return jnp.sum(tiles.astype(jnp.float32), axis=0)


def laid_out(tiles, dim):
    dims = list(tiles.shape[1:])
    dims[dim] *= tiles.shape[0]
    return jnp.moveaxis(tiles, 0, dim).reshape(dims)


def gathered_copies(array, axis, dim):
    tiles = sent_to_all(array, axis)
    return laid_out(tiles, dim)


def by_axis(array, axes):
    return functools.reduce(lax.psum, axes, array)


def head_gradient(preact, head_out, targets, label_mask):
    count = preact.shape[0]
    objectives, hidden = head_out.shape
    cube = preact.reshape(count, objectives, hidden)
    squash = jax.nn.sigmoid(cube)
    scores = jnp.sum(cube * squash * head_out[None], axis=2)
    errors = label_mask.astype(jnp.float32) * (scores - targets)
    slopes = squash * (1.0 + cube * (1.0 - squash))
    row_grad = (errors[:, :, None] * head_out[None] * slopes).astype(jnp.bfloat16)
    return row_grad.reshape(count, objectives * hidden)


def per_device(resid, norm_gain, head_in, head_bias, head_out, targets, label_mask, obj_weight):
    tok_rows = resid.shape[0]
    objectives, hidden = head_out.shape
    total_tokens = tok_rows * lax.axis_size(TOK)
    floated = resid.astype(jnp.float32)
    row_sums = over_copies(jnp.sum(floated * floated, axis=1), "tp")
    inverse = lax.rsqrt(row_sums[:, None] / D + norm_eps)
    unit = floated * inverse
    normed = (unit * norm_gain[None, :]).astype(jnp.bfloat16)
    partial_value = jnp.dot(normed, head_in, preferred_element_type=jnp.float32)
    quarter = summed_on_arrival(partial_value.astype(jnp.bfloat16), "tp", 0)
    share = quarter.shape[0]
    offset = lax.axis_index("tp") * share
    part_targets = lax.dynamic_slice_in_dim(targets, offset, share, 0)
    part_mask = lax.dynamic_slice_in_dim(label_mask, offset, share, 0)
    part_grad = head_gradient(quarter + head_bias[None, :], head_out, part_targets, part_mask)
    row_grad = gathered_copies(part_grad, "tp", 0)
    grad_float = row_grad.astype(jnp.float32)
    weight_cube = head_in.reshape(head_in.shape[0], objectives, hidden)
    gram = jnp.einsum("doh,dog->ohg", weight_cube, weight_cube, preferred_element_type=jnp.float32)
    grad_cube = grad_float.reshape(tok_rows, objectives, hidden)
    mapped = jnp.einsum("toh,ohg->tog", grad_cube, gram, precision=lax.Precision.HIGHEST)
    local_squares = jnp.sum(mapped * grad_cube, axis=(0, 2))
    squares = by_axis(local_squares, TOK_TP)
    obj_rms = jnp.sqrt(squares / (total_tokens * D) + grad_eps)
    balance = obj_weight.astype(jnp.float32) / denominator / obj_rms
    balance_cols = jnp.repeat(balance, hidden)
    pre_grad = (grad_float * balance_cols[None, :]).astype(jnp.bfloat16)
    norm_grad = lax.dot_general(
        pre_grad, head_in, (((1,), (1,)), ((), ())), preferred_element_type=jnp.float32
    )
    gain_sum, bias_sum = (
        by_axis(jnp.sum(norm_grad * unit, axis=0), TOK),
        by_axis(jnp.sum(grad_float, axis=0), TOK),
    )
    gain_grad = gain_sum / total_tokens
    head_bias_grad = bias_sum * balance_cols / total_tokens
    projection = over_copies(jnp.sum(unit * norm_gain[None, :] * norm_grad, axis=1), "tp")
    resid_grad = (
        inverse * (norm_gain[None, :] * norm_grad - unit * (projection[:, None] / D))
    ).astype(jnp.bfloat16)
    weight_term = lax.dot_general(
        normed, row_grad, (((0,), (0,)), ((), ())), preferred_element_type=jnp.float32
    )
    summed_block = lax.psum_scatter(
        weight_term.astype(jnp.bfloat16), TOK, scatter_dimension=1, tiled=True
    ).astype(jnp.float32)
    columns = summed_block.shape[1]
    col_scale = lax.dynamic_slice_in_dim(balance_cols, lax.axis_index(TOK) * columns, columns, 0)
    head_in_grad = summed_block * col_scale[None, :] / total_tokens
    return (resid_grad, gain_grad, head_in_grad, head_bias_grad)


def solution(mesh):
    finer = Mesh(mesh.devices.reshape(4, 8, 2, mesh.shape["tp"]), ("tok_0", "tok_1", "tok_2", "tp"))
    placed = (P(TOK, "tp"), P("tp"), P("tp", None), P(), P(), P(TOK, None), P(TOK, None), P())
    return jax.shard_map(
        per_device,
        mesh=finer,
        in_specs=placed,
        out_specs=(P(TOK, "tp"), P("tp"), P("tp", TOK), P()),
        check_vma=False,
    )
```

profile of v0, /device:TPU:8, one launch (start us, length us, event | category | flops | bytes accessed | tf_op | source)
XLA Modules:
  0.0 214.5 jit_solution(15858811181929445548)
XLA Ops:
  7.2 0.0 copy-start
  7.2 1.2 fusion.15
  8.4 8.5 %all_to_all.22 = f32[4,1,128]{2,1,0:T(1,128)S(1)} all-to-all(f32[4,1,128]{2,1,0:T(1,128)S(1)} %broadcast_in_dim.8), channel_id=1, replica_groups=mesh['tok_0'=4,'tok_1'=8,'tok_2'=2,'tp'=4] {'tp'}, dimensions={0} | all-to-all | bytes 4096 | tf_op jit(solution)/shard_map/all_to_all | solution.py:21
  17.0 0.0 copy-start.3
  17.0 0.0 copy-start.4
  17.0 0.0 copy-start.1
  17.0 0.0 copy-start.2
  17.0 5.7 %convolution_convert_fusion.1 = bf16[128,2048]{1,0:T(8,128)(2,1)} fusion(bf16[2048,2048]{1,0:T(8,128)(2,1)} %param.10, bf16[128,2048]{1,0:T(8,128)(2,1)} %param.8, f32[2048]{0:T(1024)} %param.9, f32[128]{0:T(128)S(1)} %add_rsqrt_fusion), kind=kOutput, calls=%fused_computation.4 | convolution fusion | flops 1075052544 | bytes 9445888 | tf_op jit(solution)/shard_map/dot_general | solution.py:79
  22.8 4.9 %all-to-all-start.1 = ((bf16[4,32,2048]{2,1,0:T(8,128)(2,1)}), bf16[4,32,2048]{2,1,0:T(8,128)(2,1)S(1)}, u32[]{:S(2)}, u32[]{:S(2)}) async-start(bf16[4,32,2048]{2,1,0:T(8,128)(2,1)} %bitcast.1), calls=%async_computation.1 | async-start | bytes 1048576 | tf_op jit(solution)/shard_map/all_to_all | solution.py:39
  27.7 0.0 reduce-scatter.2.cloned.1.call-start
  27.7 0.0 copy-done
  27.7 0.1 constant_dynamic-slice_fusion.1
  27.7 0.1 copy.41
  27.8 0.0 copy-done.5
  27.8 0.1 constant_dynamic-slice_fusion
  27.9 0.1 copy.42
  28.0 6.6 %all-to-all-done.1 = bf16[4,32,2048]{2,1,0:T(8,128)(2,1)S(1)} async-done(((bf16[4,32,2048]{2,1,0:T(8,128)(2,1)}), bf16[4,32,2048]{2,1,0:T(8,128)(2,1)S(1)}, u32[]{:S(2)}, u32[]{:S(2)}) %all-to-all-start.1) | async-done | bytes 524320 | tf_op jit(solution)/shard_map/all_to_all | solution.py:39
  34.5 0.1 convert_reduce_fusion.1
  34.7 0.0 copy-done.3
  34.7 0.2 multiply_reduce_fusion
  34.9 0.1 mul.151
  35.0 0.2 fusion.19
  35.3 10.5 %all_to_all.23 = bf16[4,32,2048]{2,1,0:T(8,128)(2,1)S(1)} all-to-all(bf16[4,32,2048]{2,1,0:T(8,128)(2,1)S(1)} %broadcast_in_dim.9), channel_id=1, replica_groups=mesh['tok_0'=4,'tok_1'=8,'tok_2'=2,'tp'=4] {'tp'}, dimensions={0} | all-to-all | bytes 1048576 | tf_op jit(solution)/shard_map/all_to_all | solution.py:21
  45.7 5.7 %convolution_convert_fusion = bf16[2048,2048]{0,1:T(8,128)(2,1)} fusion(bf16[128,2048]{1,0:T(8,128)(2,1)S(1)} %bitcast.40, bf16[128,2048]{1,0:T(8,128)(2,1)S(1)} %copy-done.1, f32[2048]{0:T(1024)S(1)} %copy-done.2, f32[128]{0:T(128)S(1)} %add_rsqrt_fusion), kind=kOutput, calls=%fused_computation.3 | convolution fusion | flops 1078984704 | bytes 9445888 | tf_op jit(solution)/shard_map/dot_general | solution.py:111
  51.4 0.0 reduce-scatter.2.cloned.1.call-update
  51.4 0.0 copy-start.6
  51.4 10.1 %fusion = f32[16,128,128]{1,2,0:T(8,128)S(1)} fusion(bf16[2048,2048]{1,0:T(8,128)(2,1)} %param.10), kind=kOutput, calls=%fused_computation | convolution fusion | flops 1073741824 | bytes 9437184 | tf_op jit(solution)/shard_map/doh,dog->ohg/dot_general | solution.py:89
  61.5 0.1 copy.46
  61.6 0.5 copy.38
  62.1 0.8 fusion.7
  62.9 10.5 %psum.70 = f32[16]{0:T(128)S(1)} all-reduce(f32[16]{0:T(128)S(1)} %fusion.7), channel_id=1, replica_groups=mesh['tok_0'=4,'tok_1'=8,'tok_2'=2,'tp'=4] {'tok_0'}, use_global_device_ids=true, to_apply=%region_5.0 | all-reduce | flops 16 | bytes 128 | tf_op jit(solution)/shard_map/psum | solution.py:55
  73.4 20.0 %psum.71 = f32[16]{0:T(128)S(1)} all-reduce(f32[16]{0:T(128)S(1)} %psum.70), channel_id=1, replica_groups=mesh['tok_0'=4,'tok_1'=8,'tok_2'=2,'tp'=4] {'tok_1'}, use_global_device_ids=true, to_apply=%region_6.0 | all-reduce | flops 16 | bytes 128 | tf_op jit(solution)/shard_map/psum | solution.py:55
  93.3 2.5 %psum.72 = f32[16]{0:T(128)S(1)} all-reduce(f32[16]{0:T(128)S(1)} %psum.71), channel_id=1, replica_groups=mesh['tok_0'=4,'tok_1'=8,'tok_2'=2,'tp'=4] {'tok_2'}, use_global_device_ids=true, to_apply=%region_7.0 | all-reduce | flops 16 | bytes 128 | tf_op jit(solution)/shard_map/psum | solution.py:55
  95.8 9.3 %psum.73 = f32[16]{0:T(128)S(1)} all-reduce(f32[16]{0:T(128)S(1)} %psum.72), channel_id=1, replica_groups=mesh['tok_0'=4,'tok_1'=8,'tok_2'=2,'tp'=4] {'tp'}, use_global_device_ids=true, to_apply=%region_8.0 | all-reduce | flops 16 | bytes 128 | tf_op jit(solution)/shard_map/psum | solution.py:55
  105.1 0.1 broadcast_bitcast_fusion
  105.2 6.7 %fusion.14 = (f32[2048]{0:T(1024)S(1)}, f32[128]{0:T(128)S(1)}, f32[128,2048]{1,0:T(8,128)S(1)}) fusion(bf16[128,2048]{1,0:T(8,128)(2,1)S(1)} %copy-done.1, f32[128]{0:T(128)S(1)} %add_rsqrt_fusion, f32[2048]{0:T(1024)S(1)} %copy-done.2, bf16[2048,2048]{1,0:T(8,128)(2,1)} %param.10, bf16[128,2048]{1,0:T(8,128)(2,1)S(1)} %bitcast.42, ...), kind=kOutput, calls=%fused_computation.19 | convolution fusion | flops 1076361088 | bytes 10511360 | tf_op jit(solution)/shard_map/dot_general | solution.py:98
  111.9 0.6 broadcast_in_dim.11
  112.5 4.4 %all-to-all-start.3 = ((f32[4,1,128]{2,1,0:T(1,128)}), f32[4,1,128]{2,1,0:T(1,128)S(1)}, u32[]{:S(2)}, u32[]{:S(2)}) async-start(f32[4,1,128]{2,1,0:T(1,128)} %broadcast_in_dim.11), calls=%async_computation.3 | async-start | bytes 4096 | tf_op jit(solution)/shard_map/all_to_all | solution.py:21
  116.8 0.1 convert_reduce_fusion
  116.9 14.3 %all-reduce.1 = (f32[2048]{0:T(1024)S(1)}, f32[2048]{0:T(1024)S(1)}) all-reduce(f32[2048]{0:T(1024)S(1)} %get-tuple-element.4, f32[2048]{0:T(1024)S(1)} %convert_reduce_fusion), channel_id=1, replica_groups=mesh['tok_0'=4,'tok_1'=8,'tok_2'=2,'tp'=4] {'tok_0'}, use_global_device_ids=true, to_apply=%region_12.0 | all-reduce | flops 4096 | bytes 32768 | tf_op jit(solution)/shard_map/psum | solution.py:55
  131.2 27.3 %all-reduce = (f32[2048]{0:T(1024)S(1)}, f32[2048]{0:T(1024)S(1)}) all-reduce(f32[2048]{0:T(1024)S(1)} %get-tuple-element.8, f32[2048]{0:T(1024)S(1)} %get-tuple-element.9), channel_id=1, replica_groups=mesh['tok_0'=4,'tok_1'=8,'tok_2'=2,'tp'=4] {'tok_1'}, use_global_device_ids=true, to_apply=%region_13.0 | all-reduce | flops 4096 | bytes 32768 | tf_op jit(solution)/shard_map/psum | solution.py:55
  158.5 3.3 %all-reduce.2 = (f32[2048]{0:T(1024)S(1)}, f32[2048]{0:T(1024)S(1)}) all-reduce(f32[2048]{0:T(1024)S(1)} %get-tuple-element.6, f32[2048]{0:T(1024)S(1)} %get-tuple-element.7), channel_id=1, replica_groups=mesh['tok_0'=4,'tok_1'=8,'tok_2'=2,'tp'=4] {'tok_2'}, use_global_device_ids=true, to_apply=%region_14.0 | all-reduce | flops 4096 | bytes 32768 | tf_op jit(solution)/shard_map/psum | solution.py:55
  161.8 0.7 multiply_multiply_fusion.1
  162.5 0.1 dynamic_slice.11
  162.5 0.0 all-to-all-done.3
  162.6 1.2 fusion.13
  163.7 42.2 %reduce-scatter.2.cloned.1.call-done = bf16[2048,32]{0,1:T(8,128)(2,1)} async-done(((bf16[2048,2048]{0,1:T(8,128)(2,1)}), bf16[2048,32]{0,1:T(8,128)(2,1)}) %reduce-scatter.2.cloned.1.call-update) | async-done | bytes 131088 | tf_op jit(solution)/shard_map/reduce_scatter | solution.py:114
  205.9 1.7 multiply_multiply_fusion
  (15 shorter events, 0.2 us)
Async XLA Ops:
  7.2 20.5 %copy-start = (s32[128,16]{0,1:T(8,128)S(1)}, s32[128,16]{0,1:T(8,128)}, u32[]{:S(2)}) copy-start(s32[128,16]{0,1:T(8,128)} %param.14) | copy-start | bytes 24580
  17.0 10.8 %copy-start.5 = (f32[128,16]{0,1:T(8,128)S(1)}, f32[128,16]{0,1:T(8,128)}, u32[]{:S(2)}) copy-start(f32[128,16]{0,1:T(8,128)} %param.13) | copy-start | bytes 24580
  17.0 17.7 %copy-start.3 = (f32[2048]{0:T(1024)S(1)}, f32[2048]{0:T(1024)}, u32[]{:S(2)}) copy-start(f32[2048]{0:T(1024)} %param.11) | copy-start | bytes 24580
  17.0 17.7 %copy-start.4 = (f32[16,128]{1,0:T(8,128)S(1)}, f32[16,128]{1,0:T(8,128)}, u32[]{:S(2)}) copy-start(f32[16,128]{1,0:T(8,128)} %param.12) | copy-start | bytes 24580
  17.0 28.7 %copy-start.1 = (bf16[128,2048]{1,0:T(8,128)(2,1)S(1)}, bf16[128,2048]{1,0:T(8,128)(2,1)}, u32[]{:S(2)}) copy-start(bf16[128,2048]{1,0:T(8,128)(2,1)} %param.8) | copy-start | bytes 1572868
  17.0 28.7 %copy-start.2 = (f32[2048]{0:T(1024)S(1)}, f32[2048]{0:T(1024)}, u32[]{:S(2)}) copy-start(f32[2048]{0:T(1024)} %param.9) | copy-start | bytes 24580
  22.8 11.8 %all-to-all-start.1 = ((bf16[4,32,2048]{2,1,0:T(8,128)(2,1)}), bf16[4,32,2048]{2,1,0:T(8,128)(2,1)S(1)}, u32[]{:S(2)}, u32[]{:S(2)}) async-start(bf16[4,32,2048]{2,1,0:T(8,128)(2,1)} %bitcast.1), calls=%async_computation.1 | async-start | bytes 1048576 | tf_op jit(solution)/shard_map/all_to_all | solution.py:39
  27.7 178.3 %reduce-scatter.2.cloned.1.call-start = ((), (), s32[]{:S(2)}) async-start(), calls=%async_computation.5 | async-start | bytes 8519680 | tf_op jit(solution)/shard_map/reduce_scatter | solution.py:114
  51.4 53.7 %copy-start.6 = (s32[16]{0:T(128)S(1)}, s32[16]{0:T(128)}, u32[]{:S(2)}) copy-start(s32[16]{0:T(128)} %param.15) | copy-start | bytes 196
  112.5 50.1 %all-to-all-start.3 = ((f32[4,1,128]{2,1,0:T(1,128)}), f32[4,1,128]{2,1,0:T(1,128)S(1)}, u32[]{:S(2)}, u32[]{:S(2)}) async-start(f32[4,1,128]{2,1,0:T(1,128)} %broadcast_in_dim.11), calls=%async_computation.3 | async-start | bytes 4096 | tf_op jit(solution)/shard_map/all_to_all | solution.py:21
Sparse Core Ops, SparseCore 0:
  51.5 154.3 reduce-scatter.1
where the time goes:
time: 215 us; the launch traced here: 214 us
  blocking collectives  106 us (49%)
  waiting for transfers between devices  48.8 us (23%)
  matrix products  28.9 us (13%)
  between operations  14.2 us (7%)
  starting transfers between devices  9.27 us (4%)
  other arithmetic  5.32 us (2%)
    psum x7, blocking collectives, by_axis(): return functools.reduce(lax.psum, axes, array)  87.1 us
    reduce_scatter x1, waiting for transfers between devices, per_device(): lax.psum_scatter(weight_term.astype(jnp.bfloat16), TOK, scatter_dimension...  42.2 us
    all_to_all x2, blocking collectives, sent_to_all(): lax.all_to_all(jnp.broadcast_to(array[None], (peers, *array.shape)), axis...  19 us
    dot_general x1, matrix products, per_device(): jnp.einsum('doh,dog->ohg', weight_cube, weight_cube, preferred_element_ty...  10.1 us
    dot_general x1, matrix products, per_device(): lax.dot_general(pre_grad, head_in, (((1,), (1,)), ((), ())), preferred_el...  6.67 us
    all_to_all x1, waiting for transfers between devices, summed_on_arrival(): tiles = lax.all_to_all(in_blocks(array, dim, peers), axis, 0, 0, tiled=True)  6.56 us
    dot_general x1, matrix products, per_device(): partial_value = jnp.dot(normed, head_in, preferred_element_type=jnp.float32)  5.72 us
    dot_general x1, matrix products, per_device(): lax.dot_general(normed, row_grad, (((0,), (0,)), ((), ())), preferred_ele...  5.66 us
  transfers between devices with their start and end apart: 3, of which 2 were waited for; matrix products, arithmetic and copies ran while one was open for 10% of the time, Pallas kernels for 0%

commit v1 on v0

v1 whole, which is shorter than its diff:
```python
import functools

import jax
import jax.numpy as jnp
from jax import lax
from jax.experimental import pallas as pl
from jax.experimental.pallas import tpu as pltpu
from jax.sharding import Mesh
from jax.sharding import PartitionSpec as P

TOK = ("tok_0", "tok_1", "tok_2")
F32 = jnp.float32
BF16 = jnp.bfloat16

norm_eps = 1e-05
grad_eps = 1e-06
denominator = 8.0

CHUNKS = 4


def remote(src, dst, send, recv, where):
    return pltpu.make_async_remote_copy(
        src_ref=src,
        dst_ref=dst,
        send_sem=send,
        recv_sem=recv,
        device_id=where,
        device_id_type=pl.DeviceIdType.MESH,
    )


def kernel(
    sizes,
    resid_hbm, head_hbm, gain_ref, bias_ref, hout_ref, tgt_ref, mask_ref, ow_ref,
    dx_hbm, gg_ref, wg_ref, bg_ref,
    resids, head, xb, part, parts_in, sums, sums_in, rg, aux, grad_t, grads, vals, sqp, msg,
    msg_y, msg_x, msg_z, gpart, gmsg, gmsg_x, gmsg_z, wt, stage, inbox, dx_buf,
    load_sem, dx_sem, y_send, y_recv, s_send, s_recv, ag_send, ag_recv, a_send, a_recv,
    r_send, r_recv, t_send, t_recv, qy_send, qy_recv, qx_send, qx_recv, qz_send, qz_recv,
    gx_send, gx_recv, gz_send, gz_recv, w_send, w_recv,
):
    X, Z, C, Y = sizes
    G = X * C
    T, DL = xb.shape
    S = T // Y
    N = head.shape[1]
    O, H = hout_ref.shape
    CW = N // CHUNKS
    D = DL * Y
    tokens = T * X * Z * C
    x, z, c, j = (lax.axis_index(a) for a in (*TOK, "tp"))
    g = x * C + c
    half = Z // 2
    hd = DL // 2

    def at_y(d):
        return {"tp": lax.rem(j + d, Y)}

    def at_xc(e):
        return {"tok_0": lax.rem(x + e // C, X), "tok_2": lax.rem(c + e % C, C)}

    def at_z(d):
        return {"tok_1": lax.rem(z + d, Z)}

    barrier = pltpu.get_barrier_semaphore()
    partners = (
        [at_y(d) for d in range(1, Y)] + [at_xc(e) for e in range(1, G)] + [at_z(d) for d in range(1, Z)]
    )
    for where in partners:
        pl.semaphore_signal(barrier, inc=1, device_id=where, device_id_type=pl.DeviceIdType.MESH)

    def rows_of(group):
        return pl.ds(pl.multiple_of(group * T, T), T)

    mine = rows_of(g)
    load = pltpu.make_async_copy(resid_hbm, resids.at[mine, :], load_sem.at[CHUNKS])
    load.start()
    for n in range(CHUNKS):
        cols = pl.ds(n * CW, CW)
        pltpu.make_async_copy(head_hbm.at[:, cols], head.at[:, cols], load_sem.at[n]).start()
    load.wait()

    total = jnp.zeros((T, 128), F32)
    for i in range(DL // 128):
        lanes = slice(i * 128, (i + 1) * 128)
        r = resids[mine, lanes].astype(F32)
        total = total + r * r
        xb[:, lanes] = (r * gain_ref[:, lanes]).astype(BF16)
    sums[...] = total

    pl.semaphore_wait(barrier, len(partners))

    east, west, twin = {"tok_0": lax.rem(x + 1, X)}, {"tok_0": lax.rem(x + X - 1, X)}, {"tok_2": 1 - c}

    def resid_copy(group, first, count, where, k):
        block = resids.at[pl.ds(pl.multiple_of(group * T + first, count), count), :]
        return remote(block, block, r_send.at[k], r_recv.at[k], where)

    g_west = lax.rem(x + X - 1, X) * C + c
    g_east = lax.rem(x + 1, X) * C + c
    g_far = lax.rem(x + 2, X) * C + c
    far = T // 2
    r_copies = [
        resid_copy(g, 0, T, east, 0),
        resid_copy(g, 0, T, west, 1),
        resid_copy(g, 0, T, twin, 2),
        resid_copy(g_west, 0, far, east, 3),
        resid_copy(g_east, far, far, west, 4),
        resid_copy(g_west, 0, T, twin, 5),
        resid_copy(g_east, 0, T, twin, 6),
        resid_copy(g_far, 0, T, twin, 7),
    ]

    def quarter(k):
        return pl.ds(pl.multiple_of(k * S, S), S)

    own = quarter(j)
    s_copies = []
    for d in range(1, Y):
        to = lax.rem(j + d, Y)
        copy = remote(
            sums.at[quarter(to), :], sums_in.at[d - 1], s_send.at[d - 1], s_recv.at[d - 1], at_y(d)
        )
        copy.start()
        s_copies.append(copy)
    y_copies = []
    for n in range(CHUNKS):
        cols = pl.ds(n * CW, CW)
        pltpu.make_async_copy(head_hbm.at[:, cols], head.at[:, cols], load_sem.at[n]).wait()
        part[:, n * CW : (n + 1) * CW] = jnp.dot(
            xb[...], head[:, n * CW : (n + 1) * CW], preferred_element_type=F32
        ).astype(BF16)
        row = []
        for d in range(1, Y):
            to = lax.rem(j + d, Y)
            copy = remote(
                part.at[quarter(to), cols],
                parts_in.at[d - 1, :, cols],
                y_send.at[d - 1, n],
                y_recv.at[d - 1, n],
                at_y(d),
            )
            copy.start()
            row.append(copy)
        y_copies.append(row)
        if n == 0:
            for k in range(3):
                r_copies[k].start()

    for copy in s_copies:
        copy.wait()
    square = sums[own, :]
    for d in range(Y - 1):
        square = square + sums_in[d]
    inv = lax.rsqrt(jnp.sum(square, axis=1, keepdims=True) / D + norm_eps)

    lane = lax.broadcasted_iota(jnp.int32, (S, 128), 1)
    tgt = tgt_ref[own, :]
    mask = mask_ref[own, :].astype(F32)
    extra = jnp.where(lane == O, inv, 0.0)
    per = O // CHUNKS
    ag_copies = []
    for n in range(CHUNKS):
        cols = pl.ds(n * CW, CW)
        for copy in y_copies[n]:
            copy.wait()
        for o in range(n * per, (n + 1) * per):
            lanes = slice(o * H, (o + 1) * H)
            value = part[own, lanes].astype(F32)
            for d in range(Y - 1):
                value = value + parts_in[d, :, lanes].astype(F32)
            value = value * inv
            cube = value + bias_ref[:, lanes]
            out = hout_ref[o : o + 1, :]
            squash = jax.nn.sigmoid(cube)
            score = jnp.sum(cube * squash * out, axis=1, keepdims=True)
            error = mask[:, o : o + 1] * (score - tgt[:, o : o + 1])
            grad = (error * out * (squash * (1.0 + cube * (1.0 - squash)))).astype(BF16)
            rg[own, lanes] = grad
            moment = jnp.sum(grad.astype(F32) * value, axis=1, keepdims=True)
            extra = jnp.where(lane == o, moment, extra)
        row = []
        for d in range(1, Y):
            block = rg.at[own, cols]
            copy = remote(block, block, ag_send.at[d - 1, n], ag_recv.at[d - 1, n], at_y(d))
            copy.start()
            row.append(copy)
        ag_copies.append(row)
    aux[own, :] = extra
    a_copies = []
    for d in range(1, Y):
        block = aux.at[own, :]
        copy = remote(block, block, a_send.at[d - 1], a_recv.at[d - 1], at_y(d))
        copy.start()
        a_copies.append(copy)

    r_copies[0].wait_recv()
    r_copies[3].start()
    r_copies[5].start()
    r_copies[1].wait_recv()
    r_copies[4].start()
    r_copies[6].start()

    for copy in a_copies:
        copy.wait()
    inverse = aux[:, O : O + 1]
    for n in range(CHUNKS):
        for copy in ag_copies[n]:
            copy.wait()
        for o in range(n * per, (n + 1) * per):
            scaled = rg[:, o * H : (o + 1) * H].astype(F32) * inverse
            flipped = jnp.transpose(scaled).astype(BF16)
            k = o * H // 32
            for b in range(H // 32):
                xx, zz, cc = (k + b) // (Z * C), (k + b) // C % Z, (k + b) % C
                grad_t[xx, zz, cc] = flipped[b * 32 : (b + 1) * 32, :]

    t_copies = []
    for e in range(1, G):
        where = at_xc(e)
        copy = remote(
            grad_t.at[where["tok_0"], :, where["tok_2"]],
            grads.at[g],
            t_send.at[e - 1],
            t_recv.at[e - 1],
            where,
        )
        copy.start()
        t_copies.append(copy)
    grads[g] = grad_t[x, :, c]

    step = 512

    def objective(o, carry):
        lanes = pl.ds(pl.multiple_of(o * H, H), H)
        lhs = rg[:, lanes]
        total = jnp.zeros((8, 128), F32)
        for i in range(DL // step):
            v = lax.dot_general(
                lhs,
                head[i * step : (i + 1) * step, lanes],
                (((1,), (1,)), ((), ())),
                preferred_element_type=F32,
            )
            vals[o, :, i * step : (i + 1) * step] = v
            for k in range(step // 128):
                w = v[:, k * 128 : (k + 1) * 128]
                total = total + jnp.sum((w * w).reshape(T // 8, 8, 128), axis=0)
        sqp[o] = total
        return carry

    lax.fori_loop(0, O, objective, 0)
    msg[0:O, :] = jnp.sum(sqp[...], axis=1)
    for o in range(O):
        msg[O + o : O + o + 1, :] = jnp.sum(
            rg[:, o * H : (o + 1) * H].astype(F32), axis=0, keepdims=True
        )

    msg_y[j] = msg[0:O, :]
    qy = []
    for d in range(1, Y):
        copy = remote(
            msg.at[0:O, :], msg_y.at[j], qy_send.at[d - 1], qy_recv.at[d - 1], at_y(d)
        )
        copy.start()
        qy.append(copy)

    r_copies[3].wait_recv()
    r_copies[4].wait_recv()
    r_copies[7].start()
    for k in (2, 5, 6, 7):
        r_copies[k].wait_recv()
    for copy in t_copies:
        copy.wait()

    wstep = 256

    def weight(i, carry):
        lanes = pl.ds(pl.multiple_of(i * wstep, wstep), wstep)
        lhs = jnp.concatenate([grads[k].reshape(Z * 32, T) for k in range(G)], axis=1)
        v = jnp.dot(lhs, resids[:, lanes], preferred_element_type=F32)
        wt[:, :, lanes] = v.reshape(Z, 32, wstep)
        return carry

    chains = ((0, 1, half), (1, -1, half), (1, 1, half - 1), (0, -1, half - 1))
    base = (0, half, 2 * half, 3 * half - 1)

    def chain_copy(k, s):
        _, direction, _ = chains[k]
        slot = base[k] + s
        return remote(
            stage.at[slot],
            inbox.at[slot],
            w_send.at[slot],
            w_recv.at[slot],
            at_z(1 if direction > 0 else Z - 1),
        )

    def chain_step(k, s):
        part_of, direction, count = chains[k]
        distance = count - s
        owner = lax.rem(z + (distance if direction > 0 else Z - distance), Z)
        lanes = slice(part_of * hd, (part_of + 1) * hd)
        value = wt[owner, :, lanes]
        if s > 0:
            chain_copy(k, s - 1).wait_recv()
            value = value + inbox[base[k] + s - 1].astype(F32)
        stage[base[k] + s] = value.astype(BF16)
        chain_copy(k, s).start()

    lax.fori_loop(0, hd // wstep, weight, 0)
    chain_step(0, 0)
    chain_step(3, 0)
    lax.fori_loop(hd // wstep, DL // wstep, weight, 0)
    chain_step(1, 0)
    chain_step(2, 0)

    def round_of(s):
        for k in range(4):
            if s < chains[k][2]:
                chain_step(k, s)

    for copy in qy:
        copy.wait()
    squares = msg_y[0]
    for k in range(1, Y):
        squares = squares + msg_y[k]
    msg[0:O, :] = squares
    msg_x[g] = msg[...]
    qx = []
    for e in range(1, G):
        copy = remote(msg, msg_x.at[g], qx_send.at[e - 1], qx_recv.at[e - 1], at_xc(e))
        copy.start()
        qx.append(copy)
    if half > 1:
        round_of(1)
    for copy in qx:
        copy.wait()
    both = msg_x[0]
    for k in range(1, G):
        both = both + msg_x[k]
    msg_z[z] = both
    qz = []
    for d in range(1, Z):
        copy = remote(msg_z.at[z], msg_z.at[z], qz_send.at[d - 1], qz_recv.at[d - 1], at_z(d))
        copy.start()
        qz.append(copy)
    if half > 2:
        round_of(2)
    for copy in qz:
        copy.wait()
    both = msg_z[0]
    for k in range(1, Z):
        both = both + msg_z[k]
    eye = lax.broadcasted_iota(jnp.int32, (O, 128), 0) == lax.broadcasted_iota(jnp.int32, (O, 128), 1)
    eye16 = lax.broadcasted_iota(jnp.int32, (O, O), 0) == lax.broadcasted_iota(jnp.int32, (O, O), 1)
    squares = jnp.sum(both[0:O, :], axis=1, keepdims=True)
    weights = jnp.sum(jnp.where(eye16, ow_ref[...].astype(F32), 0.0), axis=1, keepdims=True)
    balance = weights / denominator / jnp.sqrt(squares / (tokens * D) + grad_eps)
    balance_row = jnp.sum(jnp.where(eye, balance, 0.0), axis=0, keepdims=True)
    bg_ref[...] = both[O : 2 * O, :] * balance / tokens

    inverse = aux[:, O : O + 1]
    projection = jnp.sum(
        jnp.where(lax.broadcasted_iota(jnp.int32, (T, 128), 1) < O, aux[...] * balance_row, 0.0),
        axis=1,
        keepdims=True,
    )
    shrink = projection / D
    factors = [jnp.broadcast_to(balance[o : o + 1, :], (8, 128)) for o in range(O)]

    def combine(i, carry):
        lanes = pl.ds(pl.multiple_of(i * 128, 128), 128)
        norm = jnp.zeros((T // 8, 8, 128), F32)
        for o in range(O):
            norm = norm + vals[o, :, lanes].reshape(T // 8, 8, 128) * factors[o][None]
        norm = norm.reshape(T, 128)
        unit = resids[mine, lanes].astype(F32) * inverse
        gpart[i] = jnp.sum((norm * unit).reshape(T // 8, 8, 128), axis=0)
        dx_buf[:, lanes] = (inverse * (gain_ref[:, lanes] * norm - unit * shrink)).astype(BF16)
        return carry

    lax.fori_loop(0, DL // 128, combine, 0)
    dx_copy = pltpu.make_async_copy(dx_buf, dx_hbm, dx_sem)
    dx_copy.start()
    gmsg[...] = jnp.sum(gpart[...], axis=1)
    gmsg_x[g] = gmsg[...]
    gx = []
    for e in range(1, G):
        copy = remote(gmsg, gmsg_x.at[g], gx_send.at[e - 1], gx_recv.at[e - 1], at_xc(e))
        copy.start()
        gx.append(copy)
    for s in range(3, half):
        round_of(s)
    for copy in gx:
        copy.wait()
    both = gmsg_x[0]
    for k in range(1, G):
        both = both + gmsg_x[k]
    gmsg_z[z] = both
    gz = []
    for d in range(1, Z):
        copy = remote(gmsg_z.at[z], gmsg_z.at[z], gz_send.at[d - 1], gz_recv.at[d - 1], at_z(d))
        copy.start()
        gz.append(copy)

    k_own = (x * Z + z) * C + c
    objective_own = k_own * 32 // H
    scale = jnp.sum(
        jnp.where(lax.broadcasted_iota(jnp.int32, (O, 1), 0) == objective_own, balance, 0.0),
        axis=0,
        keepdims=True,
    )
    for part_of in range(2):
        lanes = slice(part_of * hd, (part_of + 1) * hd)
        value = wt[z, :, lanes]
        for k in range(4):
            if chains[k][0] == part_of and chains[k][2] > 0:
                chain_copy(k, chains[k][2] - 1).wait_recv()
                value = value + inbox[base[k] + chains[k][2] - 1].astype(F32)
        wg_ref[:, lanes] = value * gain_ref[:, lanes] * scale / tokens

    for copy in gz:
        copy.wait()
    both = gmsg_z[0]
    for k in range(1, Z):
        both = both + gmsg_z[k]
    gg_ref[...] = both / tokens

    for copy in r_copies:
        copy.wait_send()
    for k in range(4):
        for s in range(chains[k][2]):
            chain_copy(k, s).wait_send()
    dx_copy.wait()


def per_device(resid, norm_gain, head_in, head_bias, head_out, targets, label_mask, obj_weight):
    X, Z, C, Y = (lax.axis_size(a) for a in (*TOK, "tp"))
    G = X * C
    T, DL = resid.shape
    N = head_in.shape[1]
    O, H = head_out.shape
    S = T // Y
    CW = N // CHUNKS
    columns = N // (X * Z * C)
    slots = 2 * (Z - 1)
    any_space = pl.BlockSpec(memory_space=pl.ANY)
    vmem = pl.BlockSpec(memory_space=pltpu.VMEM)
    dma = pltpu.SemaphoreType.DMA
    V = pltpu.VMEM
    scratch = [
        V((G * T, DL), BF16),
        V((DL, N), BF16),
        V((T, DL), BF16),
        V((T, N), BF16),
        V((Y - 1, S, N), BF16),
        V((T, 128), F32),
        V((Y - 1, S, 128), F32),
        V((T, N), BF16),
        V((T, 128), F32),
        V((X, Z, C, columns, T), BF16),
        V((G, Z, columns, T), BF16),
        V((O, T, DL), F32),
        V((O, 8, 128), F32),
        V((2 * O, 128), F32),
        V((Y, O, 128), F32),
        V((G, 2 * O, 128), F32),
        V((Z, 2 * O, 128), F32),
        V((DL // 128, 8, 128), F32),
        V((DL // 128, 128), F32),
        V((G, DL // 128, 128), F32),
        V((Z, DL // 128, 128), F32),
        V((Z, columns, DL), F32),
        V((slots, columns, DL // 2), BF16),
        V((slots, columns, DL // 2), BF16),
        V((T, DL), BF16),
        dma((CHUNKS + 1,)),
        dma,
        dma((Y - 1, CHUNKS)), dma((Y - 1, CHUNKS)),
        dma((Y - 1,)), dma((Y - 1,)),
        dma((Y - 1, CHUNKS)), dma((Y - 1, CHUNKS)),
        dma((Y - 1,)), dma((Y - 1,)),
        dma((8,)), dma((8,)),
        dma((G - 1,)), dma((G - 1,)),
        dma((Y - 1,)), dma((Y - 1,)),
        dma((G - 1,)), dma((G - 1,)),
        dma((Z - 1,)), dma((Z - 1,)),
        dma((G - 1,)), dma((G - 1,)),
        dma((Z - 1,)), dma((Z - 1,)),
        dma((slots,)), dma((slots,)),
    ]
    dx, gg, wg, bg = pl.pallas_call(
        functools.partial(kernel, (X, Z, C, Y)),
        out_shape=(
            jax.ShapeDtypeStruct((T, DL), BF16),
            jax.ShapeDtypeStruct((DL // 128, 128), F32),
            jax.ShapeDtypeStruct((columns, DL), F32),
            jax.ShapeDtypeStruct((O, H), F32),
        ),
        in_specs=[any_space, any_space] + [vmem] * 6,
        out_specs=(any_space, vmem, vmem, vmem),
        scratch_shapes=scratch,
        compiler_params=pltpu.CompilerParams(
            collective_id=0, has_side_effects=True, vmem_limit_bytes=60 << 20
        ),
    )(
        resid,
        head_in,
        norm_gain.reshape(1, DL),
        head_bias.reshape(1, N),
        head_out,
        targets,
        label_mask,
        obj_weight.reshape(1, O),
    )
    return dx, gg.reshape(DL), wg.T, bg.reshape(N)


def solution(mesh):
    finer = Mesh(mesh.devices.reshape(4, 8, 2, mesh.shape["tp"]), ("tok_0", "tok_1", "tok_2", "tp"))
    placed = (P(TOK, "tp"), P("tp"), P("tp", None), P(), P(), P(TOK, None), P(TOK, None), P())
    return jax.shard_map(
        per_device,
        mesh=finer,
        in_specs=placed,
        out_specs=(P(TOK, "tp"), P("tp"), P("tp", TOK), P()),
        check_vma=False,
    )
```

time: 215 us -> 74.8 us (0.35)
  blocking collectives: 106 us -> 0 us
  Pallas kernels: 0 us -> 64.1 us
  waiting for transfers between devices: 48.8 us -> 0 us
  matrix products: 28.9 us -> 0 us
  between operations: 14.2 us -> 0.64 us
  starting transfers between devices: 9.27 us -> 0 us
  local copies, waits for them, and re-layouts: 1.88 us -> 8.99 us
  other arithmetic: 5.32 us -> 0 us
    psum x7 -> x0, blocking collectives: 87.1 us -> none  [by_axis(): return functools.reduce(lax.psum, axes, array)]
    pallas_call x0 -> x1, Pallas kernels: none -> 64.1 us  [per_device(): pl.pallas_call(functools.partial(kernel, (X, Z, C, Y)), out_shape=(jax.Sh...]
    reduce_scatter x1 -> x0, waiting for transfers between devices: 42.2 us -> none  [per_device(): lax.psum_scatter(weight_term.astype(jnp.bfloat16), TOK, scatter_dimension...]
    dot_general x5 -> x0, matrix products: 28.9 us -> none  [the longest x1 10.1 us: per_device(): jnp.einsum('doh,dog->ohg', weight_cube, weight_cube, preferred_element_ty...]
    all_to_all x2 -> x0, blocking collectives: 19 us -> none  [sent_to_all(): lax.all_to_all(jnp.broadcast_to(array[None], (peers, *array.shape)), axis...]
    all_to_all x2 -> x0, starting transfers between devices: 9.27 us -> none  [the longest x1 4.9 us: summed_on_arrival(): tiles = lax.all_to_all(in_blocks(array, dim, peers), axis, 0, 0, tiled=True)]
    unnamed x18 -> x6, local copies, waits for them, and re-layouts: 0.36 us -> 8.99 us
    all_to_all x2 -> x0, waiting for transfers between devices: 6.57 us -> none  [the longest x1 6.56 us: summed_on_arrival(): tiles = lax.all_to_all(in_blocks(array, dim, peers), axis, 0, 0, tiled=True)]
  transfers between devices with their start and end apart: 3 -> 0, of which waited for: 2 -> 0; matrix products, arithmetic and copies ran while one was open for 10% -> 0% of each run, Pallas kernels for 0% -> 0%
where the time goes in v1:
time: 74.8 us; the launch traced here: 73.7 us
  Pallas kernels  64.1 us (86%)
  local copies, waits for them, and re-layouts  8.99 us (12%)
    pallas_call x1, Pallas kernels, per_device(): pl.pallas_call(functools.partial(kernel, (X, Z, C, Y)), out_shape=(jax.Sh...  64.1 us
    unnamed x6, local copies, waits for them, and re-layouts  8.99 us

profile of v1, /device:TPU:8, one launch (start us, length us, event | category | flops | bytes accessed | tf_op | source)
XLA Modules:
  0.0 73.7 jit_solution(7210114312805512754)
XLA Ops:
  0.6 1.4 %copy.12.tgt_ref = f32[128,16]{1,0:T(8,128)} copy(f32[128,16]{0,1:T(8,128)} %param.13) | data formatting | bytes 16384 | tf_op args[5]
  2.1 1.4 %copy.13.mask_ref = s32[128,16]{1,0:T(8,128)} copy(s32[128,16]{0,1:T(8,128)} %param.14) | data formatting | bytes 16384 | tf_op args[6]
  3.5 64.1 %shard_map.111 = (bf16[128,2048]{1,0:T(8,128)(2,1)}, f32[16,128]{1,0:T(8,128)}, f32[32,2048]{1,0:T(8,128)}, f32[16,128]{1,0:T(8,128)}) custom-call(bf16[128,2048]{1,0:T(8,128)(2,1)} %resid_hbm.1, bf16[2048,2048]{1,0:T(8,128)(2,1)} %head_hbm.1, f32[1,2048]{1,0:T(1,128)} %bitcast.9, f32[1,2048]{1,0:T(1,128)} %bitcast.10, f32[16,128]{1,0:T(8,128)} %hout_ref.1, ...), custom_call_target="tpu_custom_call" | custom-call | tf_op jit(solution)/shard_map/pallas_call | solution.py:494
  67.6 1.9 %copy.18 = bf16[128,2048]{1,0:T(8,128)(2,1)} copy(bf16[128,2048]{1,0:T(8,128)(2,1)} %get-tuple-element.16) | data formatting | bytes 1048576
  69.5 1.3 %copy.19 = f32[2048]{0:T(1024)} copy(f32[2048]{0:T(1024)} %bitcast.8) | data formatting | bytes 16384
  70.8 1.7 %copy.20 = f32[2048,32]{0,1:T(8,128)} copy(f32[2048,32]{0,1:T(8,128)} %bitcast.6) | data formatting | bytes 524288
  72.4 1.3 %copy.21 = f32[2048]{0:T(1024)} copy(f32[2048]{0:T(1024)} %bitcast.7) | data formatting | bytes 16384

commit v2 on v1

--- a/solution.py
+++ b/solution.py
@@ -32,11 +32,12 @@
 
 def kernel(
     sizes,
-    resid_hbm, head_hbm, gain_ref, bias_ref, hout_ref, tgt_ref, mask_ref, ow_ref,
-    dx_hbm, gg_ref, wg_ref, bg_ref,
-    resids, head, xb, part, parts_in, sums, sums_in, rg, aux, grad_t, grads, vals, sqp, msg,
-    msg_y, msg_x, msg_z, gpart, gmsg, gmsg_x, gmsg_z, wt, stage, inbox, dx_buf,
-    load_sem, dx_sem, y_send, y_recv, s_send, s_recv, ag_send, ag_recv, a_send, a_recv,
+    resid_hbm, head_hbm, gain_hbm, bias_hbm, hout_hbm, tgt_hbm, mask_hbm, ow_hbm,
+    dx_ref, gg_ref, wg_ref, bg_ref,
+    gain_ref, bias_ref, hout_ref, tgt_ref, mask_ref, ow_ref,
+    tgt_t, mask_t, resids, head, xb, part, parts_in, sums, sums_in, rg, aux, grad_t, grads, vals, sqp, msg,
+    msg_y, msg_x, msg_z, gpart, gmsg, gmsg_x, gmsg_z, wt, stage, inbox,
+    load_sem, small_sem, y_send, y_recv, s_send, s_recv, ag_send, ag_recv, a_send, a_recv,
     r_send, r_recv, t_send, t_recv, qy_send, qy_recv, qx_send, qx_recv, qz_send, qz_recv,
     gx_send, gx_recv, gz_send, gz_recv, w_send, w_recv,
 ):
@@ -76,9 +77,28 @@
     mine = rows_of(g)
     load = pltpu.make_async_copy(resid_hbm, resids.at[mine, :], load_sem.at[CHUNKS])
     load.start()
+    small = [
+        pltpu.make_async_copy(src, dst, small_sem.at[k])
+        for k, (src, dst) in enumerate(
+            (
+                (gain_hbm, gain_ref),
+                (bias_hbm, bias_ref),
+                (hout_hbm, hout_ref),
+                (tgt_hbm, tgt_ref),
+                (mask_hbm, mask_ref),
+                (ow_hbm, ow_ref),
+            )
+        )
+    ]
+    for copy in small:
+        copy.start()
     for n in range(CHUNKS):
         cols = pl.ds(n * CW, CW)
         pltpu.make_async_copy(head_hbm.at[:, cols], head.at[:, cols], load_sem.at[n]).start()
+    for copy in small:
+        copy.wait()
+    tgt_t[...] = jnp.transpose(tgt_ref[...])
+    mask_t[...] = jnp.transpose(mask_ref[...].astype(F32))
     load.wait()
 
     total = jnp.zeros((T, 128), F32)
@@ -102,14 +122,16 @@
     g_far = lax.rem(x + 2, X) * C + c
     far = T // 2
     r_copies = [
-        resid_copy(g, 0, T, east, 0),
-        resid_copy(g, 0, T, west, 1),
-        resid_copy(g, 0, T, twin, 2),
-        resid_copy(g_west, 0, far, east, 3),
-        resid_copy(g_east, far, far, west, 4),
-        resid_copy(g_west, 0, T, twin, 5),
-        resid_copy(g_east, 0, T, twin, 6),
-        resid_copy(g_far, 0, T, twin, 7),
+        resid_copy(g, 0, far, east, 0),
+        resid_copy(g, far, far, west, 1),
+        resid_copy(g, far, far, east, 2),
+        resid_copy(g, 0, far, west, 3),
+        resid_copy(g, 0, T, twin, 4),
+        resid_copy(g_west, 0, far, east, 5),
+        resid_copy(g_east, far, far, west, 6),
+        resid_copy(g_west, 0, T, twin, 7),
+        resid_copy(g_east, 0, T, twin, 8),
+        resid_copy(g_far, 0, T, twin, 9),
     ]
 
     def quarter(k):
@@ -145,7 +167,7 @@
             row.append(copy)
         y_copies.append(row)
         if n == 0:
-            for k in range(3):
+            for k in range(5):
                 r_copies[k].start()
 
     for copy in s_copies:
@@ -156,8 +178,8 @@
     inv = lax.rsqrt(jnp.sum(square, axis=1, keepdims=True) / D + norm_eps)
 
     lane = lax.broadcasted_iota(jnp.int32, (S, 128), 1)
-    tgt = tgt_ref[own, :]
-    mask = mask_ref[own, :].astype(F32)
+    tgt = tgt_t[own, :]
+    mask = mask_t[own, :]
     extra = jnp.where(lane == O, inv, 0.0)
     per = O // CHUNKS
     ag_copies = []
@@ -196,10 +218,8 @@
         a_copies.append(copy)
 
     r_copies[0].wait_recv()
-    r_copies[3].start()
     r_copies[5].start()
     r_copies[1].wait_recv()
-    r_copies[4].start()
     r_copies[6].start()
 
     for copy in a_copies:
@@ -229,6 +249,11 @@
         copy.start()
         t_copies.append(copy)
     grads[g] = grad_t[x, :, c]
+
+    r_copies[2].wait_recv()
+    r_copies[7].start()
+    r_copies[3].wait_recv()
+    r_copies[8].start()
 
     step = 512
 
@@ -266,10 +291,22 @@
         copy.start()
         qy.append(copy)
 
-    r_copies[3].wait_recv()
-    r_copies[4].wait_recv()
-    r_copies[7].start()
-    for k in (2, 5, 6, 7):
+    r_copies[5].wait_recv()
+    r_copies[6].wait_recv()
+    r_copies[9].start()
+    for copy in qy:
+        copy.wait()
+    squares = msg_y[0]
+    for k in range(1, Y):
+        squares = squares + msg_y[k]
+    msg[0:O, :] = squares
+    msg_x[g] = msg[...]
+    qx = []
+    for e in range(1, G):
+        copy = remote(msg, msg_x.at[g], qx_send.at[e - 1], qx_recv.at[e - 1], at_xc(e))
+        copy.start()
+        qx.append(copy)
+    for k in (4, 7, 8, 9):
         r_copies[k].wait_recv()
     for copy in t_copies:
         copy.wait()
@@ -312,29 +349,7 @@
     lax.fori_loop(0, hd // wstep, weight, 0)
     chain_step(0, 0)
     chain_step(3, 0)
-    lax.fori_loop(hd // wstep, DL // wstep, weight, 0)
-    chain_step(1, 0)
-    chain_step(2, 0)
-
-    def round_of(s):
-        for k in range(4):
-            if s < chains[k][2]:
-                chain_step(k, s)
-
-    for copy in qy:
-        copy.wait()
-    squares = msg_y[0]
-    for k in range(1, Y):
-        squares = squares + msg_y[k]
-    msg[0:O, :] = squares
-    msg_x[g] = msg[...]
-    qx = []
-    for e in range(1, G):
-        copy = remote(msg, msg_x.at[g], qx_send.at[e - 1], qx_recv.at[e - 1], at_xc(e))
-        copy.start()
-        qx.append(copy)
-    if half > 1:
-        round_of(1)
+
     for copy in qx:
         copy.wait()
     both = msg_x[0]
@@ -346,8 +361,18 @@
         copy = remote(msg_z.at[z], msg_z.at[z], qz_send.at[d - 1], qz_recv.at[d - 1], at_z(d))
         copy.start()
         qz.append(copy)
-    if half > 2:
-        round_of(2)
+
+    lax.fori_loop(hd // wstep, DL // wstep, weight, 0)
+    chain_step(1, 0)
+    chain_step(2, 0)
+
+    def round_of(s):
+        for k in range(4):
+            if s < chains[k][2]:
+                chain_step(k, s)
+
+    if half > 1:
+        round_of(1)
     for copy in qz:
         copy.wait()
     both = msg_z[0]
@@ -378,12 +403,10 @@
         norm = norm.reshape(T, 128)
         unit = resids[mine, lanes].astype(F32) * inverse
         gpart[i] = jnp.sum((norm * unit).reshape(T // 8, 8, 128), axis=0)
-        dx_buf[:, lanes] = (inverse * (gain_ref[:, lanes] * norm - unit * shrink)).astype(BF16)
+        dx_ref[:, lanes] = (inverse * (gain_ref[:, lanes] * norm - unit * shrink)).astype(BF16)
         return carry
 
     lax.fori_loop(0, DL // 128, combine, 0)
-    dx_copy = pltpu.make_async_copy(dx_buf, dx_hbm, dx_sem)
-    dx_copy.start()
     gmsg[...] = jnp.sum(gpart[...], axis=1)
     gmsg_x[g] = gmsg[...]
     gx = []
@@ -391,8 +414,8 @@
         copy = remote(gmsg, gmsg_x.at[g], gx_send.at[e - 1], gx_recv.at[e - 1], at_xc(e))
         copy.start()
         gx.append(copy)
-    for s in range(3, half):
-        round_of(s)
+    if half > 2:
+        round_of(2)
     for copy in gx:
         copy.wait()
     both = gmsg_x[0]
@@ -404,6 +427,9 @@
         copy = remote(gmsg_z.at[z], gmsg_z.at[z], gz_send.at[d - 1], gz_recv.at[d - 1], at_z(d))
         copy.start()
         gz.append(copy)
+
+    for s in range(3, half):
+        round_of(s)
 
     k_own = (x * Z + z) * C + c
     objective_own = k_own * 32 // H
@@ -433,7 +459,13 @@
     for k in range(4):
         for s in range(chains[k][2]):
             chain_copy(k, s).wait_send()
-    dx_copy.wait()
+
+
+def settle(dx_ref, gg_ref, wg_ref, bg_ref, dx_out, gg_out, wg_out, bg_out):
+    dx_out[...] = dx_ref[...]
+    gg_out[...] = gg_ref[...]
+    wg_out[...] = wg_ref[...]
+    bg_out[...] = bg_ref[...]
 
 
 def per_device(resid, norm_gain, head_in, head_bias, head_out, targets, label_mask, obj_weight):
@@ -446,11 +478,19 @@
     CW = N // CHUNKS
     columns = N // (X * Z * C)
     slots = 2 * (Z - 1)
-    any_space = pl.BlockSpec(memory_space=pl.ANY)
+    hbm = pl.BlockSpec(memory_space=pltpu.HBM)
     vmem = pl.BlockSpec(memory_space=pltpu.VMEM)
     dma = pltpu.SemaphoreType.DMA
     V = pltpu.VMEM
     scratch = [
+        V((1, DL), F32),
+        V((1, N), F32),
+        V((O, H), F32),
+        V((O, T), F32),
+        V((O, T), jnp.int32),
+        V((1, O), jnp.int32),
+        V((T, O), F32),
+        V((T, O), F32),
         V((G * T, DL), BF16),
         V((DL, N), BF16),
         V((T, DL), BF16),
@@ -475,14 +515,12 @@
         V((Z, columns, DL), F32),
         V((slots, columns, DL // 2), BF16),
         V((slots, columns, DL // 2), BF16),
-        V((T, DL), BF16),
-        dma((CHUNKS + 1,)),
-        dma,
+        dma((CHUNKS + 1,)), dma((6,)),
         dma((Y - 1, CHUNKS)), dma((Y - 1, CHUNKS)),
         dma((Y - 1,)), dma((Y - 1,)),
         dma((Y - 1, CHUNKS)), dma((Y - 1, CHUNKS)),
         dma((Y - 1,)), dma((Y - 1,)),
-        dma((8,)), dma((8,)),
+        dma((10,)), dma((10,)),
         dma((G - 1,)), dma((G - 1,)),
         dma((Y - 1,)), dma((Y - 1,)),
         dma((G - 1,)), dma((G - 1,)),
@@ -499,22 +537,34 @@
             jax.ShapeDtypeStruct((columns, DL), F32),
             jax.ShapeDtypeStruct((O, H), F32),
         ),
-        in_specs=[any_space, any_space] + [vmem] * 6,
-        out_specs=(any_space, vmem, vmem, vmem),
+        in_specs=[hbm] * 8,
+        out_specs=(vmem,) * 4,
         scratch_shapes=scratch,
         compiler_params=pltpu.CompilerParams(
-            collective_id=0, has_side_effects=True, vmem_limit_bytes=60 << 20
+            collective_id=0, has_side_effects=True, vmem_limit_bytes=48 << 20
         ),
     )(
-        resid,
-        head_in,
-        norm_gain.reshape(1, DL),
-        head_bias.reshape(1, N),
-        head_out,
-        targets,
-        label_mask,
-        obj_weight.reshape(1, O),
+        *(
+            pltpu.with_memory_space_constraint(a, pltpu.HBM)
+            for a in (
+                resid,
+                head_in,
+                norm_gain.reshape(1, DL),
+                head_bias.reshape(1, N),
+                head_out,
+                targets.T,
+                label_mask.T,
+                obj_weight.reshape(1, O),
+            )
+        )
     )
+    dx, gg, wg, bg = pl.pallas_call(
+        settle,
+        out_shape=tuple(jax.ShapeDtypeStruct(a.shape, a.dtype) for a in (dx, gg, wg, bg)),
+        in_specs=[vmem] * 4,
+        out_specs=(vmem,) * 4,
+        compiler_params=pltpu.CompilerParams(vmem_limit_bytes=4 << 20),
+    )(dx, gg, wg, bg)
     return dx, gg.reshape(DL), wg.T, bg.reshape(N)
 
 

time: 74.8 us -> 60.3 us (0.81)
  local copies, waits for them, and re-layouts: 8.99 us -> 0 us
  Pallas kernels: 64.1 us -> 58.6 us
    unnamed x6 -> x0, local copies, waits for them, and re-layouts: 8.99 us -> none
    pallas_call x1, Pallas kernels: 64.1 us -> 57.6 us  [per_device(): pl.pallas_call(functools.partial(kernel, (X, Z, C, Y)), out_shape=(jax.Sh...]
    pallas_call x0 -> x1, Pallas kernels: none -> 0.94 us  [per_device(): pl.pallas_call(settle, out_shape=tuple((jax.ShapeDtypeStruct(a.shape, a.d...]
where the time goes in v2:
time: 60.3 us; the launch traced here: 59.2 us
  Pallas kernels  58.6 us (97%)
  between operations  0.64 us (1%)
    pallas_call x1, Pallas kernels, per_device(): pl.pallas_call(functools.partial(kernel, (X, Z, C, Y)), out_shape=(jax.Sh...  57.6 us

profile of v2, /device:TPU:8, one launch (start us, length us, event | category | flops | bytes accessed | tf_op | source)
XLA Modules:
  0.0 59.2 jit_solution(17540306294775312037)
XLA Ops:
  0.6 57.6 %shard_map.111 = (bf16[128,2048]{1,0:T(8,128)(2,1)S(1)}, f32[16,128]{1,0:T(8,128)S(1)}, f32[32,2048]{1,0:T(8,128)S(1)}, f32[16,128]{1,0:T(8,128)S(1)}) custom-call(bf16[128,2048]{1,0:T(8,128)(2,1)} %resid_hbm.1, bf16[2048,2048]{1,0:T(8,128)(2,1)} %head_hbm.1, f32[1,2048]{1,0:T(1,128)} %bitcast.8, f32[1,2048]{1,0:T(1,128)} %bitcast.9, f32[16,128]{1,0:T(8,128)} %hout_hbm.1, ...), custom_call_target="tpu_custom_call" | custom-call | tf_op jit(solution)/shard_map/pallas_call | solution.py:532
  58.3 0.9 %shard_map.112 = (bf16[128,2048]{1,0:T(8,128)(2,1)}, f32[16,128]{1,0:T(8,128)}, f32[32,2048]{1,0:T(8,128)}, f32[16,128]{1,0:T(8,128)}) custom-call(bf16[128,2048]{1,0:T(8,128)(2,1)S(1)} %get-tuple-element.12.dx_ref, f32[16,128]{1,0:T(8,128)S(1)} %get-tuple-element.13.gg_ref, f32[32,2048]{1,0:T(8,128)S(1)} %get-tuple-element.14.wg_ref, ...), custom_call_target="tpu_custom_call" | custom-call | tf_op jit(solution)/shard_map/pallas_call | solution.py:561

commit v3 on v2

--- a/solution.py
+++ b/solution.py
@@ -16,7 +16,8 @@
 grad_eps = 1e-06
 denominator = 8.0
 
-CHUNKS = 4
+STEPS = (2, 1, 3, 0)
+CHUNKS = len(STEPS)
 
 
 def remote(src, dst, send, recv, where):
@@ -35,10 +36,10 @@
     resid_hbm, head_hbm, gain_hbm, bias_hbm, hout_hbm, tgt_hbm, mask_hbm, ow_hbm,
     dx_ref, gg_ref, wg_ref, bg_ref,
     gain_ref, bias_ref, hout_ref, tgt_ref, mask_ref, ow_ref,
-    tgt_t, mask_t, resids, head, xb, part, parts_in, sums, sums_in, rg, aux, grad_t, grads, vals, sqp, msg,
-    msg_y, msg_x, msg_z, gpart, gmsg, gmsg_x, gmsg_z, wt, stage, inbox,
-    load_sem, small_sem, y_send, y_recv, s_send, s_recv, ag_send, ag_recv, a_send, a_recv,
-    r_send, r_recv, t_send, t_recv, qy_send, qy_recv, qx_send, qx_recv, qz_send, qz_recv,
+    tgt_t, mask_t, resids, head, xb, part, parts_in, sums, sums_in, rg, aux, inverses, grad_t, grads, vals, sqp,
+    msg_b, msg_y, msg_x, msg_z, gpart, gmsg, gmsg_x, gmsg_z, wt, stage, inbox,
+    load_sem, small_sem, y_send, y_recv, s_send, s_recv, ag_send, ag_recv, a_send, a_recv, i_send, i_recv,
+    r_send, r_recv, t_send, t_recv, qy_send, qy_recv, qx_send, qx_recv, qz_send, qz_recv, qb_send, qb_recv,
     gx_send, gx_recv, gz_send, gz_recv, w_send, w_recv,
 ):
     X, Z, C, Y = sizes
@@ -92,23 +93,19 @@
     ]
     for copy in small:
         copy.start()
-    for n in range(CHUNKS):
-        cols = pl.ds(n * CW, CW)
-        pltpu.make_async_copy(head_hbm.at[:, cols], head.at[:, cols], load_sem.at[n]).start()
-    for copy in small:
-        copy.wait()
-    tgt_t[...] = jnp.transpose(tgt_ref[...])
-    mask_t[...] = jnp.transpose(mask_ref[...].astype(F32))
+    def block_of(d):
+        return lax.rem(x + d, X)
+
+    def cols_of(d):
+        return pl.ds(pl.multiple_of(block_of(d) * CW, CW), CW)
+
+    head_loads = {
+        d: pltpu.make_async_copy(head_hbm.at[:, cols_of(d)], head.at[:, cols_of(d)], load_sem.at[d])
+        for d in STEPS
+    }
+    for d in STEPS:
+        head_loads[d].start()
     load.wait()
-
-    total = jnp.zeros((T, 128), F32)
-    for i in range(DL // 128):
-        lanes = slice(i * 128, (i + 1) * 128)
-        r = resids[mine, lanes].astype(F32)
-        total = total + r * r
-        xb[:, lanes] = (r * gain_ref[:, lanes]).astype(BF16)
-    sums[...] = total
-
     pl.semaphore_wait(barrier, len(partners))
 
     east, west, twin = {"tok_0": lax.rem(x + 1, X)}, {"tok_0": lax.rem(x + X - 1, X)}, {"tok_2": 1 - c}
@@ -134,86 +131,109 @@
         resid_copy(g_far, 0, T, twin, 9),
     ]
 
+    for k in range(5):
+        r_copies[k].start()
+
+    for copy in small:
+        copy.wait()
+    tgt_t[...] = jnp.transpose(tgt_ref[...])
+    mask_t[...] = jnp.transpose(mask_ref[...].astype(F32))
+    total = jnp.zeros((T, 128), F32)
+    for i in range(DL // 128):
+        lanes = slice(i * 128, (i + 1) * 128)
+        r = resids[mine, lanes].astype(F32)
+        total = total + r * r
+        xb[:, lanes] = (r * gain_ref[:, lanes]).astype(BF16)
+    sums[...] = total
+
     def quarter(k):
         return pl.ds(pl.multiple_of(k * S, S), S)
 
     own = quarter(j)
     s_copies = []
-    for d in range(1, Y):
-        to = lax.rem(j + d, Y)
+    for k in range(1, Y):
+        to = lax.rem(j + k, Y)
         copy = remote(
-            sums.at[quarter(to), :], sums_in.at[d - 1], s_send.at[d - 1], s_recv.at[d - 1], at_y(d)
+            sums.at[quarter(to), :], sums_in.at[k - 1], s_send.at[k - 1], s_recv.at[k - 1], at_y(k)
         )
         copy.start()
         s_copies.append(copy)
-    y_copies = []
-    for n in range(CHUNKS):
-        cols = pl.ds(n * CW, CW)
-        pltpu.make_async_copy(head_hbm.at[:, cols], head.at[:, cols], load_sem.at[n]).wait()
-        part[:, n * CW : (n + 1) * CW] = jnp.dot(
-            xb[...], head[:, n * CW : (n + 1) * CW], preferred_element_type=F32
-        ).astype(BF16)
-        row = []
-        for d in range(1, Y):
-            to = lax.rem(j + d, Y)
+    y_copies = {}
+    for d in STEPS:
+        cols = cols_of(d)
+        head_loads[d].wait()
+        part[:, cols] = jnp.dot(xb[...], head[:, cols], preferred_element_type=F32).astype(BF16)
+        y_copies[d] = []
+        for k in range(1, Y):
+            to = lax.rem(j + k, Y)
             copy = remote(
                 part.at[quarter(to), cols],
-                parts_in.at[d - 1, :, cols],
-                y_send.at[d - 1, n],
-                y_recv.at[d - 1, n],
-                at_y(d),
+                parts_in.at[k - 1, :, cols],
+                y_send.at[k - 1, d],
+                y_recv.at[k - 1, d],
+                at_y(k),
             )
             copy.start()
-            row.append(copy)
-        y_copies.append(row)
-        if n == 0:
-            for k in range(5):
-                r_copies[k].start()
+            y_copies[d].append(copy)
 
     for copy in s_copies:
         copy.wait()
     square = sums[own, :]
-    for d in range(Y - 1):
-        square = square + sums_in[d]
+    for k in range(Y - 1):
+        square = square + sums_in[k]
     inv = lax.rsqrt(jnp.sum(square, axis=1, keepdims=True) / D + norm_eps)
+    inverses[own, :] = jnp.broadcast_to(inv, (S, 128))
+    i_copies = []
+    for k in range(1, Y):
+        block = inverses.at[own, :]
+        copy = remote(block, block, i_send.at[k - 1], i_recv.at[k - 1], at_y(k))
+        copy.start()
+        i_copies.append(copy)
 
     lane = lax.broadcasted_iota(jnp.int32, (S, 128), 1)
+    lane_o = lax.broadcasted_iota(jnp.int32, (S, O), 1)
     tgt = tgt_t[own, :]
     mask = mask_t[own, :]
-    extra = jnp.where(lane == O, inv, 0.0)
+    extra = jnp.zeros((S, 128), F32)
     per = O // CHUNKS
-    ag_copies = []
-    for n in range(CHUNKS):
-        cols = pl.ds(n * CW, CW)
-        for copy in y_copies[n]:
+
+    def lanes_of(d, i):
+        return pl.ds(pl.multiple_of(block_of(d) * CW + i * H, H), H)
+
+    ag_copies = {}
+    for d in STEPS:
+        for copy in y_copies[d]:
             copy.wait()
-        for o in range(n * per, (n + 1) * per):
-            lanes = slice(o * H, (o + 1) * H)
+        for i in range(per):
+            lanes = lanes_of(d, i)
+            o = block_of(d) * per + i
             value = part[own, lanes].astype(F32)
-            for d in range(Y - 1):
-                value = value + parts_in[d, :, lanes].astype(F32)
+            for k in range(Y - 1):
+                value = value + parts_in[k, :, lanes].astype(F32)
             value = value * inv
             cube = value + bias_ref[:, lanes]
-            out = hout_ref[o : o + 1, :]
+            out = hout_ref[pl.ds(o, 1), :]
             squash = jax.nn.sigmoid(cube)
             score = jnp.sum(cube * squash * out, axis=1, keepdims=True)
-            error = mask[:, o : o + 1] * (score - tgt[:, o : o + 1])
+            here = lane_o == o
+            label = jnp.sum(jnp.where(here, mask, 0.0), axis=1, keepdims=True)
+            target = jnp.sum(jnp.where(here, tgt, 0.0), axis=1, keepdims=True)
+            error = label * (score - target)
             grad = (error * out * (squash * (1.0 + cube * (1.0 - squash)))).astype(BF16)
             rg[own, lanes] = grad
             moment = jnp.sum(grad.astype(F32) * value, axis=1, keepdims=True)
             extra = jnp.where(lane == o, moment, extra)
-        row = []
-        for d in range(1, Y):
-            block = rg.at[own, cols]
-            copy = remote(block, block, ag_send.at[d - 1, n], ag_recv.at[d - 1, n], at_y(d))
+        ag_copies[d] = []
+        for k in range(1, Y):
+            block = rg.at[own, cols_of(d)]
+            copy = remote(block, block, ag_send.at[k - 1, d], ag_recv.at[k - 1, d], at_y(k))
             copy.start()
-            row.append(copy)
-        ag_copies.append(row)
+            ag_copies[d].append(copy)
     aux[own, :] = extra
     a_copies = []
-    for d in range(1, Y):
+    for k in range(1, Y):
         block = aux.at[own, :]
-        copy = remote(block, block, a_send.at[d - 1], a_recv.at[d - 1], at_y(d))
+        copy = remote(block, block, a_send.at[k - 1], a_recv.at[k - 1], at_y(k))
         copy.start()
         a_copies.append(copy)
 
@@ -222,88 +242,100 @@
     r_copies[1].wait_recv()
     r_copies[6].start()
 
-    for copy in a_copies:
-        copy.wait()
-    inverse = aux[:, O : O + 1]
-    for n in range(CHUNKS):
-        for copy in ag_copies[n]:
+    step = 512
+
+    def objective(d, i, carry):
+        lanes = lanes_of(d, i)
+        o = block_of(d) * per + i
+        lhs = rg[:, lanes]
+        total = jnp.zeros((8, 128), F32)
+        for k in range(DL // step):
+            v = lax.dot_general(
+                lhs,
+                head[k * step : (k + 1) * step, lanes],
+                (((1,), (1,)), ((), ())),
+                preferred_element_type=F32,
+            )
+            vals[o, :, k * step : (k + 1) * step] = v
+            for q in range(step // 128):
+                w = v[:, q * 128 : (q + 1) * 128]
+                total = total + jnp.sum((w * w).reshape(T // 8, 8, 128), axis=0)
+        sqp[o] = total
+        return carry
+
+    for copy in i_copies:
+        copy.wait()
+    t_copies = []
+    for d in STEPS:
+        for copy in ag_copies[d]:
             copy.wait()
-        for o in range(n * per, (n + 1) * per):
-            scaled = rg[:, o * H : (o + 1) * H].astype(F32) * inverse
+        for i in range(per):
+            scaled = rg[:, lanes_of(d, i)].astype(F32) * inverses[...]
             flipped = jnp.transpose(scaled).astype(BF16)
-            k = o * H // 32
             for b in range(H // 32):
-                xx, zz, cc = (k + b) // (Z * C), (k + b) // C % Z, (k + b) % C
-                grad_t[xx, zz, cc] = flipped[b * 32 : (b + 1) * 32, :]
-
-    t_copies = []
-    for e in range(1, G):
-        where = at_xc(e)
-        copy = remote(
-            grad_t.at[where["tok_0"], :, where["tok_2"]],
-            grads.at[g],
-            t_send.at[e - 1],
-            t_recv.at[e - 1],
-            where,
-        )
-        copy.start()
-        t_copies.append(copy)
-    grads[g] = grad_t[x, :, c]
+                k = i * (H // 32) + b
+                grad_t[d, k // C, k % C] = flipped[b * 32 : (b + 1) * 32, :]
+        for e in range(d * C, (d + 1) * C):
+            where = at_xc(e)
+            if e == 0:
+                grads[g] = grad_t[0, :, c]
+                continue
+            copy = remote(
+                grad_t.at[d, :, where["tok_2"]],
+                grads.at[g],
+                t_send.at[e - 1],
+                t_recv.at[e - 1],
+                where,
+            )
+            copy.start()
+            t_copies.append(copy)
+        lax.fori_loop(0, per, functools.partial(objective, d), 0)
+
+    eye = lax.broadcasted_iota(jnp.int32, (O, 128), 0) == lax.broadcasted_iota(jnp.int32, (O, 128), 1)
+    local = jnp.sum(jnp.sum(sqp[...], axis=1), axis=1, keepdims=True)
+    msg_y[j] = jnp.broadcast_to(jnp.sum(jnp.where(eye, local, 0.0), axis=0, keepdims=True), (8, 128))
+    qy = []
+    for d in range(1, Y):
+        copy = remote(msg_y.at[j], msg_y.at[j], qy_send.at[d - 1], qy_recv.at[d - 1], at_y(d))
+        copy.start()
+        qy.append(copy)
+    share_o = O // Y
+    rows8 = lax.broadcasted_iota(jnp.int32, (8, 128), 0)
+    bias_rows = jnp.zeros((8, 128), F32)
+    for k in range(share_o):
+        lanes = pl.ds(pl.multiple_of((j * share_o + k) * H, H), H)
+        line = jnp.sum(rg[:, lanes].astype(F32), axis=0, keepdims=True)
+        bias_rows = jnp.where(rows8 == k + 1, line, bias_rows)
 
     r_copies[2].wait_recv()
     r_copies[7].start()
     r_copies[3].wait_recv()
     r_copies[8].start()
-
-    step = 512
-
-    def objective(o, carry):
-        lanes = pl.ds(pl.multiple_of(o * H, H), H)
-        lhs = rg[:, lanes]
-        total = jnp.zeros((8, 128), F32)
-        for i in range(DL // step):
-            v = lax.dot_general(
-                lhs,
-                head[i * step : (i + 1) * step, lanes],
-                (((1,), (1,)), ((), ())),
-                preferred_element_type=F32,
-            )
-            vals[o, :, i * step : (i + 1) * step] = v
-            for k in range(step // 128):
-                w = v[:, k * 128 : (k + 1) * 128]
-                total = total + jnp.sum((w * w).reshape(T // 8, 8, 128), axis=0)
-        sqp[o] = total
-        return carry
-
-    lax.fori_loop(0, O, objective, 0)
-    msg[0:O, :] = jnp.sum(sqp[...], axis=1)
-    for o in range(O):
-        msg[O + o : O + o + 1, :] = jnp.sum(
-            rg[:, o * H : (o + 1) * H].astype(F32), axis=0, keepdims=True
-        )
-
-    msg_y[j] = msg[0:O, :]
-    qy = []
-    for d in range(1, Y):
-        copy = remote(
-            msg.at[0:O, :], msg_y.at[j], qy_send.at[d - 1], qy_recv.at[d - 1], at_y(d)
-        )
-        copy.start()
-        qy.append(copy)
-
+    for copy in qy:
+        copy.wait()
+    squares = msg_y[0]
+    for k in range(1, Y):
+        squares = squares + msg_y[k]
+    msg_z[z] = jnp.where(rows8 == 0, squares, bias_rows)
+    qz = []
+    for k in range(1, Z):
+        copy = remote(msg_z.at[z], msg_z.at[z], qz_send.at[k - 1], qz_recv.at[k - 1], at_z(k))
+        copy.start()
+        qz.append(copy)
     r_copies[5].wait_recv()
     r_copies[6].wait_recv()
     r_copies[9].start()
-    for copy in qy:
-        copy.wait()
-    squares = msg_y[0]
-    for k in range(1, Y):
-        squares = squares + msg_y[k]
-    msg[0:O, :] = squares
-    msg_x[g] = msg[...]
+    for copy in a_copies:
+        copy.wait()
+    for copy in qz:
+        copy.wait()
+    both = msg_z[0]
+    for k in range(1, Z):
+        both = both + msg_z[k]
+    msg_x[g] = both
     qx = []
     for e in range(1, G):
-        copy = remote(msg, msg_x.at[g], qx_send.at[e - 1], qx_recv.at[e - 1], at_xc(e))
+        copy = remote(msg_x.at[g], msg_x.at[g], qx_send.at[e - 1], qx_recv.at[e - 1], at_xc(e))
         copy.start()
         qx.append(copy)
     for k in (4, 7, 8, 9):
@@ -350,43 +382,33 @@
     chain_step(0, 0)
     chain_step(3, 0)
 
+    lax.fori_loop(hd // wstep, DL // wstep, weight, 0)
+    chain_step(1, 0)
+    chain_step(2, 0)
+
+    def round_of(s, which=(0, 3, 1, 2)):
+        for k in which:
+            if s < chains[k][2]:
+                chain_step(k, s)
+
     for copy in qx:
         copy.wait()
     both = msg_x[0]
     for k in range(1, G):
         both = both + msg_x[k]
-    msg_z[z] = both
-    qz = []
-    for d in range(1, Z):
-        copy = remote(msg_z.at[z], msg_z.at[z], qz_send.at[d - 1], qz_recv.at[d - 1], at_z(d))
-        copy.start()
-        qz.append(copy)
-
-    lax.fori_loop(hd // wstep, DL // wstep, weight, 0)
-    chain_step(1, 0)
-    chain_step(2, 0)
-
-    def round_of(s):
-        for k in range(4):
-            if s < chains[k][2]:
-                chain_step(k, s)
-
-    if half > 1:
-        round_of(1)
-    for copy in qz:
-        copy.wait()
-    both = msg_z[0]
-    for k in range(1, Z):
-        both = both + msg_z[k]
-    eye = lax.broadcasted_iota(jnp.int32, (O, 128), 0) == lax.broadcasted_iota(jnp.int32, (O, 128), 1)
+    msg_b[j] = both
+    qb = []
+    for d in range(1, Y):
+        copy = remote(msg_b.at[j], msg_b.at[j], qb_send.at[d - 1], qb_recv.at[d - 1], at_y(d))
+        copy.start()
+        qb.append(copy)
     eye16 = lax.broadcasted_iota(jnp.int32, (O, O), 0) == lax.broadcasted_iota(jnp.int32, (O, O), 1)
-    squares = jnp.sum(both[0:O, :], axis=1, keepdims=True)
+    squares = jnp.sum(jnp.where(eye, both[0:1, :], 0.0), axis=1, keepdims=True)
     weights = jnp.sum(jnp.where(eye16, ow_ref[...].astype(F32), 0.0), axis=1, keepdims=True)
     balance = weights / denominator / jnp.sqrt(squares / (tokens * D) + grad_eps)
     balance_row = jnp.sum(jnp.where(eye, balance, 0.0), axis=0, keepdims=True)
-    bg_ref[...] = both[O : 2 * O, :] * balance / tokens
-
-    inverse = aux[:, O : O + 1]
+
+    inverse = inverses[...]
     projection = jnp.sum(
         jnp.where(lax.broadcasted_iota(jnp.int32, (T, 128), 1) < O, aux[...] * balance_row, 0.0),
         axis=1,
@@ -406,7 +428,11 @@
         dx_ref[:, lanes] = (inverse * (gain_ref[:, lanes] * norm - unit * shrink)).astype(BF16)
         return carry
 
-    lax.fori_loop(0, DL // 128, combine, 0)
+    pieces = DL // 128
+    lax.fori_loop(0, pieces // 2, combine, 0)
+    if half > 1:
+        round_of(1, (0, 3))
+    lax.fori_loop(pieces // 2, pieces, combine, 0)
     gmsg[...] = jnp.sum(gpart[...], axis=1)
     gmsg_x[g] = gmsg[...]
     gx = []
@@ -414,6 +440,8 @@
         copy = remote(gmsg, gmsg_x.at[g], gx_send.at[e - 1], gx_recv.at[e - 1], at_xc(e))
         copy.start()
         gx.append(copy)
+    if half > 1:
+        round_of(1, (1, 2))
     if half > 2:
         round_of(2)
     for copy in gx:
@@ -447,6 +475,12 @@
                 value = value + inbox[base[k] + chains[k][2] - 1].astype(F32)
         wg_ref[:, lanes] = value * gain_ref[:, lanes] * scale / tokens
 
+    for copy in qb:
+        copy.wait()
+    for k in range(Y):
+        for i in range(share_o):
+            o = k * share_o + i
+            bg_ref[o : o + 1, :] = msg_b[k, i + 1 : i + 2, :] * balance[o : o + 1, :] / tokens
     for copy in gz:
         copy.wait()
     both = gmsg_z[0]
@@ -500,14 +534,15 @@
         V((Y - 1, S, 128), F32),
         V((T, N), BF16),
         V((T, 128), F32),
+        V((T, 128), F32),
         V((X, Z, C, columns, T), BF16),
         V((G, Z, columns, T), BF16),
         V((O, T, DL), F32),
         V((O, 8, 128), F32),
-        V((2 * O, 128), F32),
-        V((Y, O, 128), F32),
-        V((G, 2 * O, 128), F32),
-        V((Z, 2 * O, 128), F32),
+        V((Y, 8, 128), F32),
+        V((Y, 8, 128), F32),
+        V((G, 8, 128), F32),
+        V((Z, 8, 128), F32),
         V((DL // 128, 8, 128), F32),
         V((DL // 128, 128), F32),
         V((G, DL // 128, 128), F32),
@@ -520,11 +555,13 @@
         dma((Y - 1,)), dma((Y - 1,)),
         dma((Y - 1, CHUNKS)), dma((Y - 1, CHUNKS)),
         dma((Y - 1,)), dma((Y - 1,)),
+        dma((Y - 1,)), dma((Y - 1,)),
         dma((10,)), dma((10,)),
         dma((G - 1,)), dma((G - 1,)),
         dma((Y - 1,)), dma((Y - 1,)),
         dma((G - 1,)), dma((G - 1,)),
         dma((Z - 1,)), dma((Z - 1,)),
+        dma((Y - 1,)), dma((Y - 1,)),
         dma((G - 1,)), dma((G - 1,)),
         dma((Z - 1,)), dma((Z - 1,)),
         dma((slots,)), dma((slots,)),

time: 60.3 us -> 56.1 us (0.930)
  Pallas kernels: 58.6 us -> 54.9 us
    pallas_call x1, Pallas kernels: 57.6 us -> 54 us  [per_device(): pl.pallas_call(functools.partial(kernel, (X, Z, C, Y)), out_shape=(jax.Sh...]
where the time goes in v3:
time: 56.1 us; the launch traced here: 55.6 us
  Pallas kernels  54.9 us (98%)
  between operations  0.64 us (1%)
    pallas_call x1, Pallas kernels, per_device(): pl.pallas_call(functools.partial(kernel, (X, Z, C, Y)), out_shape=(jax.Sh...  54 us

profile of v3, /device:TPU:8, one launch (start us, length us, event | category | flops | bytes accessed | tf_op | source)
XLA Modules:
  0.0 55.6 jit_solution(15662885073098276807)
XLA Ops:
  0.6 54.0 %shard_map.111 = (bf16[128,2048]{1,0:T(8,128)(2,1)S(1)}, f32[16,128]{1,0:T(8,128)S(1)}, f32[32,2048]{1,0:T(8,128)S(1)}, f32[16,128]{1,0:T(8,128)S(1)}) custom-call(bf16[128,2048]{1,0:T(8,128)(2,1)} %resid_hbm.1, bf16[2048,2048]{1,0:T(8,128)(2,1)} %head_hbm.1, f32[1,2048]{1,0:T(1,128)} %bitcast.8, f32[1,2048]{1,0:T(1,128)} %bitcast.9, f32[16,128]{1,0:T(8,128)} %hout_hbm.1, ...), custom_call_target="tpu_custom_call" | custom-call | tf_op jit(solution)/shard_map/pallas_call | solution.py:569
  54.6 0.9 %shard_map.112 = (bf16[128,2048]{1,0:T(8,128)(2,1)}, f32[16,128]{1,0:T(8,128)}, f32[32,2048]{1,0:T(8,128)}, f32[16,128]{1,0:T(8,128)}) custom-call(bf16[128,2048]{1,0:T(8,128)(2,1)S(1)} %get-tuple-element.12.dx_ref, f32[16,128]{1,0:T(8,128)S(1)} %get-tuple-element.13.gg_ref, f32[32,2048]{1,0:T(8,128)S(1)} %get-tuple-element.14.wg_ref, ...), custom_call_target="tpu_custom_call" | custom-call | tf_op jit(solution)/shard_map/pallas_call | solution.py:598

commit v4 on v3

--- a/solution.py
+++ b/solution.py
@@ -18,6 +18,7 @@
 
 STEPS = (2, 1, 3, 0)
 CHUNKS = len(STEPS)
+PARTS = 4
 
 
 def remote(src, dst, send, recv, where):
@@ -37,9 +38,9 @@
     dx_ref, gg_ref, wg_ref, bg_ref,
     gain_ref, bias_ref, hout_ref, tgt_ref, mask_ref, ow_ref,
     tgt_t, mask_t, resids, head, xb, part, parts_in, sums, sums_in, rg, aux, inverses, grad_t, grads, vals, sqp,
-    msg_b, msg_y, msg_x, msg_z, gpart, gmsg, gmsg_x, gmsg_z, wt, stage, inbox,
+    msg_b, msg_p, msg_x, msg_z, gpart, gmsg, gmsg_x, gmsg_z, wt, stage, inbox,
     load_sem, small_sem, y_send, y_recv, s_send, s_recv, ag_send, ag_recv, a_send, a_recv, i_send, i_recv,
-    r_send, r_recv, t_send, t_recv, qy_send, qy_recv, qx_send, qx_recv, qz_send, qz_recv, qb_send, qb_recv,
+    r_send, r_recv, t_send, t_recv, qp_send, qp_recv, qx_send, qx_recv, qz_send, qz_recv, qb_send, qb_recv,
     gx_send, gx_recv, gz_send, gz_recv, w_send, w_recv,
 ):
     X, Z, C, Y = sizes
@@ -54,7 +55,7 @@
     x, z, c, j = (lax.axis_index(a) for a in (*TOK, "tp"))
     g = x * C + c
     half = Z // 2
-    hd = DL // 2
+    hd = DL // PARTS
 
     def at_y(d):
         return {"tp": lax.rem(j + d, Y)}
@@ -64,13 +65,6 @@
 
     def at_z(d):
         return {"tok_1": lax.rem(z + d, Z)}
-
-    barrier = pltpu.get_barrier_semaphore()
-    partners = (
-        [at_y(d) for d in range(1, Y)] + [at_xc(e) for e in range(1, G)] + [at_z(d) for d in range(1, Z)]
-    )
-    for where in partners:
-        pl.semaphore_signal(barrier, inc=1, device_id=where, device_id_type=pl.DeviceIdType.MESH)
 
     def rows_of(group):
         return pl.ds(pl.multiple_of(group * T, T), T)
@@ -91,8 +85,9 @@
             )
         )
     ]
-    for copy in small:
-        copy.start()
+    small[0].start()
+    for copy in small[1:]:
+        copy.start(priority=1)
     def block_of(d):
         return lax.rem(x + d, X)
 
@@ -105,6 +100,15 @@
     }
     for d in STEPS:
         head_loads[d].start()
+
+    def at_plane(k):
+        return {**at_y(k // G), **at_xc(k % G)}
+
+    barrier = pltpu.get_barrier_semaphore()
+    partners = [at_plane(k) for k in range(1, Y * G)] + [at_z(d) for d in range(1, Z)]
+    for where in partners:
+        pl.semaphore_signal(barrier, inc=1, device_id=where, device_id_type=pl.DeviceIdType.MESH)
+
     load.wait()
     pl.semaphore_wait(barrier, len(partners))
 
@@ -134,10 +138,7 @@
     for k in range(5):
         r_copies[k].start()
 
-    for copy in small:
-        copy.wait()
-    tgt_t[...] = jnp.transpose(tgt_ref[...])
-    mask_t[...] = jnp.transpose(mask_ref[...].astype(F32))
+    small[0].wait()
     total = jnp.zeros((T, 128), F32)
     for i in range(DL // 128):
         lanes = slice(i * 128, (i + 1) * 128)
@@ -176,6 +177,10 @@
             copy.start()
             y_copies[d].append(copy)
 
+    for copy in small[1:]:
+        copy.wait()
+    tgt_t[...] = jnp.transpose(tgt_ref[...])
+    mask_t[...] = jnp.transpose(mask_ref[...].astype(F32))
     for copy in s_copies:
         copy.wait()
     square = sums[own, :]
@@ -293,12 +298,7 @@
 
     eye = lax.broadcasted_iota(jnp.int32, (O, 128), 0) == lax.broadcasted_iota(jnp.int32, (O, 128), 1)
     local = jnp.sum(jnp.sum(sqp[...], axis=1), axis=1, keepdims=True)
-    msg_y[j] = jnp.broadcast_to(jnp.sum(jnp.where(eye, local, 0.0), axis=0, keepdims=True), (8, 128))
-    qy = []
-    for d in range(1, Y):
-        copy = remote(msg_y.at[j], msg_y.at[j], qy_send.at[d - 1], qy_recv.at[d - 1], at_y(d))
-        copy.start()
-        qy.append(copy)
+    squares = jnp.sum(jnp.where(eye, local, 0.0), axis=0, keepdims=True)
     share_o = O // Y
     rows8 = lax.broadcasted_iota(jnp.int32, (8, 128), 0)
     bias_rows = jnp.zeros((8, 128), F32)
@@ -307,21 +307,17 @@
         line = jnp.sum(rg[:, lanes].astype(F32), axis=0, keepdims=True)
         bias_rows = jnp.where(rows8 == k + 1, line, bias_rows)
 
+    msg_z[z] = jnp.where(rows8 == 0, squares, bias_rows)
+    qz = []
+    for k in range(1, Z):
+        copy = remote(msg_z.at[z], msg_z.at[z], qz_send.at[k - 1], qz_recv.at[k - 1], at_z(k))
+        copy.start()
+        qz.append(copy)
+
     r_copies[2].wait_recv()
     r_copies[7].start()
     r_copies[3].wait_recv()
     r_copies[8].start()
-    for copy in qy:
-        copy.wait()
-    squares = msg_y[0]
-    for k in range(1, Y):
-        squares = squares + msg_y[k]
-    msg_z[z] = jnp.where(rows8 == 0, squares, bias_rows)
-    qz = []
-    for k in range(1, Z):
-        copy = remote(msg_z.at[z], msg_z.at[z], qz_send.at[k - 1], qz_recv.at[k - 1], at_z(k))
-        copy.start()
-        qz.append(copy)
     r_copies[5].wait_recv()
     r_copies[6].wait_recv()
     r_copies[9].start()
@@ -332,7 +328,14 @@
     both = msg_z[0]
     for k in range(1, Z):
         both = both + msg_z[k]
+    seat = j * G + g
+    msg_p[seat] = both[0:1, :]
     msg_x[g] = both
+    qp = []
+    for k in range(1, Y * G):
+        copy = remote(msg_p.at[seat], msg_p.at[seat], qp_send.at[k - 1], qp_recv.at[k - 1], at_plane(k))
+        copy.start()
+        qp.append(copy)
     qx = []
     for e in range(1, G):
         copy = remote(msg_x.at[g], msg_x.at[g], qx_send.at[e - 1], qx_recv.at[e - 1], at_xc(e))
@@ -341,69 +344,54 @@
     for k in (4, 7, 8, 9):
         r_copies[k].wait_recv()
     for copy in t_copies:
-        copy.wait()
-
-    wstep = 256
-
-    def weight(i, carry):
-        lanes = pl.ds(pl.multiple_of(i * wstep, wstep), wstep)
+        copy.wait_recv()
+
+    def weight(p):
+        lanes = slice(p * hd, (p + 1) * hd)
         lhs = jnp.concatenate([grads[k].reshape(Z * 32, T) for k in range(G)], axis=1)
         v = jnp.dot(lhs, resids[:, lanes], preferred_element_type=F32)
-        wt[:, :, lanes] = v.reshape(Z, 32, wstep)
-        return carry
-
-    chains = ((0, 1, half), (1, -1, half), (1, 1, half - 1), (0, -1, half - 1))
-    base = (0, half, 2 * half, 3 * half - 1)
-
-    def chain_copy(k, s):
-        _, direction, _ = chains[k]
-        slot = base[k] + s
+        wt[:, :, lanes] = v.reshape(Z, 32, hd)
+
+    def count_of(p, way):
+        return half - (p + way) % 2
+
+    def slot_of(p, way, s):
+        return (p * (2 * half - 1)) + (half - p % 2 if way else 0) + s
+
+    def chain_copy(p, way, s):
+        slot = slot_of(p, way, s)
         return remote(
             stage.at[slot],
             inbox.at[slot],
             w_send.at[slot],
             w_recv.at[slot],
-            at_z(1 if direction > 0 else Z - 1),
+            at_z(Z - 1 if way else 1),
         )
 
-    def chain_step(k, s):
-        part_of, direction, count = chains[k]
-        distance = count - s
-        owner = lax.rem(z + (distance if direction > 0 else Z - distance), Z)
-        lanes = slice(part_of * hd, (part_of + 1) * hd)
-        value = wt[owner, :, lanes]
-        if s > 0:
-            chain_copy(k, s - 1).wait_recv()
-            value = value + inbox[base[k] + s - 1].astype(F32)
-        stage[base[k] + s] = value.astype(BF16)
-        chain_copy(k, s).start()
-
-    lax.fori_loop(0, hd // wstep, weight, 0)
-    chain_step(0, 0)
-    chain_step(3, 0)
-
-    lax.fori_loop(hd // wstep, DL // wstep, weight, 0)
-    chain_step(1, 0)
-    chain_step(2, 0)
-
-    def round_of(s, which=(0, 3, 1, 2)):
-        for k in which:
-            if s < chains[k][2]:
-                chain_step(k, s)
-
-    for copy in qx:
-        copy.wait()
-    both = msg_x[0]
-    for k in range(1, G):
-        both = both + msg_x[k]
-    msg_b[j] = both
-    qb = []
-    for d in range(1, Y):
-        copy = remote(msg_b.at[j], msg_b.at[j], qb_send.at[d - 1], qb_recv.at[d - 1], at_y(d))
-        copy.start()
-        qb.append(copy)
+    def chain_step(p, s):
+        lanes = slice(p * hd, (p + 1) * hd)
+        for way in range(2):
+            count = count_of(p, way)
+            if s < count:
+                distance = count - s
+                owner = lax.rem(z + (Z - distance if way else distance), Z)
+                value = wt[owner, :, lanes]
+                if s > 0:
+                    chain_copy(p, way, s - 1).wait_recv()
+                    value = value + inbox[slot_of(p, way, s - 1)].astype(F32)
+                stage[slot_of(p, way, s)] = value.astype(BF16)
+                chain_copy(p, way, s).start()
+
+    for p in range(PARTS):
+        weight(p)
+        chain_step(p, 0)
+    for copy in qp:
+        copy.wait()
+    squares = msg_p[0]
+    for k in range(1, Y * G):
+        squares = squares + msg_p[k]
     eye16 = lax.broadcasted_iota(jnp.int32, (O, O), 0) == lax.broadcasted_iota(jnp.int32, (O, O), 1)
-    squares = jnp.sum(jnp.where(eye, both[0:1, :], 0.0), axis=1, keepdims=True)
+    squares = jnp.sum(jnp.where(eye, squares, 0.0), axis=1, keepdims=True)
     weights = jnp.sum(jnp.where(eye16, ow_ref[...].astype(F32), 0.0), axis=1, keepdims=True)
     balance = weights / denominator / jnp.sqrt(squares / (tokens * D) + grad_eps)
     balance_row = jnp.sum(jnp.where(eye, balance, 0.0), axis=0, keepdims=True)
@@ -429,10 +417,10 @@
         return carry
 
     pieces = DL // 128
-    lax.fori_loop(0, pieces // 2, combine, 0)
-    if half > 1:
-        round_of(1, (0, 3))
-    lax.fori_loop(pieces // 2, pieces, combine, 0)
+    for p in range(PARTS):
+        lax.fori_loop(p * pieces // PARTS, (p + 1) * pieces // PARTS, combine, 0)
+        if half > 1:
+            chain_step(p, 1)
     gmsg[...] = jnp.sum(gpart[...], axis=1)
     gmsg_x[g] = gmsg[...]
     gx = []
@@ -440,10 +428,20 @@
         copy = remote(gmsg, gmsg_x.at[g], gx_send.at[e - 1], gx_recv.at[e - 1], at_xc(e))
         copy.start()
         gx.append(copy)
-    if half > 1:
-        round_of(1, (1, 2))
     if half > 2:
-        round_of(2)
+        for p in range(PARTS):
+            chain_step(p, 2)
+    for copy in qx:
+        copy.wait()
+    both = msg_x[0]
+    for k in range(1, G):
+        both = both + msg_x[k]
+    msg_b[j] = both
+    qb = []
+    for k in range(1, Y):
+        copy = remote(msg_b.at[j], msg_b.at[j], qb_send.at[k - 1], qb_recv.at[k - 1], at_y(k))
+        copy.start()
+        qb.append(copy)
     for copy in gx:
         copy.wait()
     both = gmsg_x[0]
@@ -457,7 +455,8 @@
         gz.append(copy)
 
     for s in range(3, half):
-        round_of(s)
+        for p in range(PARTS):
+            chain_step(p, s)
 
     k_own = (x * Z + z) * C + c
     objective_own = k_own * 32 // H
@@ -466,15 +465,15 @@
         axis=0,
         keepdims=True,
     )
-    for part_of in range(2):
-        lanes = slice(part_of * hd, (part_of + 1) * hd)
+    for p in range(PARTS):
+        lanes = slice(p * hd, (p + 1) * hd)
         value = wt[z, :, lanes]
-        for k in range(4):
-            if chains[k][0] == part_of and chains[k][2] > 0:
-                chain_copy(k, chains[k][2] - 1).wait_recv()
-                value = value + inbox[base[k] + chains[k][2] - 1].astype(F32)
+        for way in range(2):
+            count = count_of(p, way)
+            if count > 0:
+                chain_copy(p, way, count - 1).wait_recv()
+                value = value + inbox[slot_of(p, way, count - 1)].astype(F32)
         wg_ref[:, lanes] = value * gain_ref[:, lanes] * scale / tokens
-
     for copy in qb:
         copy.wait()
     for k in range(Y):
@@ -488,11 +487,12 @@
         both = both + gmsg_z[k]
     gg_ref[...] = both / tokens
 
-    for copy in r_copies:
+    for copy in r_copies + t_copies:
         copy.wait_send()
-    for k in range(4):
-        for s in range(chains[k][2]):
-            chain_copy(k, s).wait_send()
+    for p in range(PARTS):
+        for way in range(2):
+            for s in range(count_of(p, way)):
+                chain_copy(p, way, s).wait_send()
 
 
 def settle(dx_ref, gg_ref, wg_ref, bg_ref, dx_out, gg_out, wg_out, bg_out):
@@ -511,7 +511,7 @@
     S = T // Y
     CW = N // CHUNKS
     columns = N // (X * Z * C)
-    slots = 2 * (Z - 1)
+    slots = PARTS * (Z - 1)
     hbm = pl.BlockSpec(memory_space=pltpu.HBM)
     vmem = pl.BlockSpec(memory_space=pltpu.VMEM)
     dma = pltpu.SemaphoreType.DMA
@@ -540,7 +540,7 @@
         V((O, T, DL), F32),
         V((O, 8, 128), F32),
         V((Y, 8, 128), F32),
-        V((Y, 8, 128), F32),
+        V((Y * G, 1, 128), F32),
         V((G, 8, 128), F32),
         V((Z, 8, 128), F32),
         V((DL // 128, 8, 128), F32),
@@ -548,8 +548,8 @@
         V((G, DL // 128, 128), F32),
         V((Z, DL // 128, 128), F32),
         V((Z, columns, DL), F32),
-        V((slots, columns, DL // 2), BF16),
-        V((slots, columns, DL // 2), BF16),
+        V((slots, columns, DL // PARTS), BF16),
+        V((slots, columns, DL // PARTS), BF16),
         dma((CHUNKS + 1,)), dma((6,)),
         dma((Y - 1, CHUNKS)), dma((Y - 1, CHUNKS)),
         dma((Y - 1,)), dma((Y - 1,)),
@@ -558,7 +558,7 @@
         dma((Y - 1,)), dma((Y - 1,)),
         dma((10,)), dma((10,)),
         dma((G - 1,)), dma((G - 1,)),
-        dma((Y - 1,)), dma((Y - 1,)),
+        dma((Y * G - 1,)), dma((Y * G - 1,)),
         dma((G - 1,)), dma((G - 1,)),
         dma((Z - 1,)), dma((Z - 1,)),
         dma((Y - 1,)), dma((Y - 1,)),

time: 56.1 us -> 55 us (0.980)
  Pallas kernels: 54.9 us -> 53.4 us
    pallas_call x1, Pallas kernels: 54 us -> 52.5 us  [per_device(): pl.pallas_call(functools.partial(kernel, (X, Z, C, Y)), out_shape=(jax.Sh...]
where the time goes in v4:
time: 55 us; the launch traced here: 54 us
  Pallas kernels  53.4 us (97%)
  between operations  0.64 us (1%)
    pallas_call x1, Pallas kernels, per_device(): pl.pallas_call(functools.partial(kernel, (X, Z, C, Y)), out_shape=(jax.Sh...  52.5 us

profile of v4, /device:TPU:8, one launch (start us, length us, event | category | flops | bytes accessed | tf_op | source)
XLA Modules:
  0.0 54.0 jit_solution(9678182576435565819)
XLA Ops:
  0.6 52.5 %shard_map.111 = (bf16[128,2048]{1,0:T(8,128)(2,1)S(1)}, f32[16,128]{1,0:T(8,128)S(1)}, f32[32,2048]{1,0:T(8,128)S(1)}, f32[16,128]{1,0:T(8,128)S(1)}) custom-call(bf16[128,2048]{1,0:T(8,128)(2,1)} %resid_hbm.1, bf16[2048,2048]{1,0:T(8,128)(2,1)} %head_hbm.1, f32[1,2048]{1,0:T(1,128)} %bitcast.8, f32[1,2048]{1,0:T(1,128)} %bitcast.9, f32[16,128]{1,0:T(8,128)} %hout_hbm.1, ...), custom_call_target="tpu_custom_call" | custom-call | tf_op jit(solution)/shard_map/pallas_call | solution.py:569
  53.1 0.9 %shard_map.112 = (bf16[128,2048]{1,0:T(8,128)(2,1)}, f32[16,128]{1,0:T(8,128)}, f32[32,2048]{1,0:T(8,128)}, f32[16,128]{1,0:T(8,128)}) custom-call(bf16[128,2048]{1,0:T(8,128)(2,1)S(1)} %get-tuple-element.12.dx_ref, f32[16,128]{1,0:T(8,128)S(1)} %get-tuple-element.13.gg_ref, f32[32,2048]{1,0:T(8,128)S(1)} %get-tuple-element.14.wg_ref, ...), custom_call_target="tpu_custom_call" | custom-call | tf_op jit(solution)/shard_map/pallas_call | solution.py:598
